TPU v7x, 128 devices: a whole 4x4x4 slice. The times are simulated.
128 devices in a mesh: ty: 2 (over core), tx: 64 (over z, y, x).
Axes of the slice: x: 4, y: 4, z: 4, core: 2. Of those that a mesh axis runs over, the one named last changes fastest.
Arguments:
- w_one: float32 [64, 2, 6, 128, 512], P('tx', 'ty')
- w_two: float32 [64, 2, 6, 512, 128], P('tx', 'ty')
- inputs: bfloat16 [64, 2, 8, 1024, 128], P('tx', 'ty')
- targets: bfloat16 [64, 2, 8, 1024, 128], P('tx', 'ty')
Outputs:
- output 1: float32 [64, 2, 6, 128, 512], P('tx', 'ty')
- output 2: float32 [64, 2, 6, 512, 128], P('tx', 'ty')
- output 3: float32 [64, 2, 8], P('tx', 'ty')
All inputs are finite; a program needn't handle non-finite values.
Results may differ from a plain program's by a relative error of at most 0.00442233.
Values are sent between devices in bfloat16 or wider.
A program may use at most 1 GiB of HBM per device.

v0:
```python
import jax
import jax.numpy as jnp
from jax import lax
from jax.sharding import PartitionSpec as P

NORM_EPS = 1e-6


def rms_float(hid_f):
    return hid_f * lax.rsqrt(jnp.mean(hid_f * hid_f, axis=-1, keepdims=True) + NORM_EPS)


def local_grads(cast_one, cast_two, step_acts, step_goals):
    layers = cast_one.shape[0]
    hidden = step_acts
    saved_list = []
    for layer_idx in range(layers):
        hid_f = hidden.astype(jnp.float32)
        normed_f, norm_back = jax.vjp(rms_float, hid_f)
        normed = normed_f.astype(jnp.bfloat16)
        pre_act = jnp.dot(normed, cast_one[layer_idx], preferred_element_type=jnp.float32)
        gelu_f, gelu_back = jax.vjp(jax.nn.gelu, pre_act)
        hidden_act = gelu_f.astype(jnp.bfloat16)
        mlp_out = jnp.dot(hidden_act, cast_two[layer_idx], preferred_element_type=jnp.float32)
        hidden = (hid_f + mlp_out).astype(jnp.bfloat16)
        saved_list.append((normed, hidden_act, norm_back, gelu_back))
    error_term = hidden.astype(jnp.float32) - step_goals.astype(jnp.float32)
    step_loss = jnp.mean(error_term * error_term)
    d_hidden = (error_term * (2.0 / error_term.size)).astype(jnp.bfloat16)
    grads_one = []
    grads_two = []
    for layer_idx in reversed(range(layers)):
        normed, hidden_act, norm_back, gelu_back = saved_list[layer_idx]
        grads_two.append(jnp.einsum("bf,bd->fd", hidden_act, d_hidden, preferred_element_type=jnp.float32).astype(jnp.bfloat16))
        d_act = jnp.einsum("bd,fd->bf", d_hidden, cast_two[layer_idx], preferred_element_type=jnp.float32).astype(jnp.bfloat16)
        (d_pre,) = gelu_back(d_act.astype(jnp.float32))
        d_pre_b = d_pre.astype(jnp.bfloat16)
        grads_one.append(jnp.einsum("bd,bf->df", normed, d_pre_b, preferred_element_type=jnp.float32).astype(jnp.bfloat16))
        if layer_idx > 0:
            d_normed = jnp.einsum("bf,df->bd", d_pre_b, cast_one[layer_idx], preferred_element_type=jnp.float32).astype(jnp.bfloat16)
            (d_norm_in,) = norm_back(d_normed.astype(jnp.float32))
            d_hidden = (d_hidden.astype(jnp.float32) + d_norm_in).astype(jnp.bfloat16)
    return step_loss, jnp.stack(grads_one[::-1]), jnp.stack(grads_two[::-1])


def neighbour_perms(grid_size):
    from_prev = [(src_idx, (src_idx + 1) % grid_size) for src_idx in range(grid_size)]
    from_next = [(src_idx, (src_idx - 1) % grid_size) for src_idx in range(grid_size)]
    return from_prev, from_next


def solution(mesh):
    prev_x, next_x = neighbour_perms(mesh.shape["tx"])
    prev_y, next_y = neighbour_perms(mesh.shape["ty"])
    routes = [("tx", prev_x), ("tx", next_x), ("ty", prev_y), ("ty", next_y)]

    def gossip(master, cast_copy):
        received = [lax.ppermute(cast_copy, axis_name, perm_pairs) for axis_name, perm_pairs in routes]
        mix_sum = master
        for recv_copy in received:
            mix_sum = mix_sum + recv_copy.astype(jnp.float32)
        return mix_sum / 5.0

    def device_train(w_one, w_two, inputs, targets):
        p_one = w_one[0, 0]
        p_two = w_two[0, 0]
        learn_rate = p_one.shape[1] / (p_one.shape[2] * p_one.shape[0])
        loss_list = []
        for step_idx in range(inputs.shape[2]):
            cast_one = p_one.astype(jnp.bfloat16)
            cast_two = p_two.astype(jnp.bfloat16)
            step_loss, g_one, g_two = local_grads(cast_one, cast_two, inputs[0, 0, step_idx], targets[0, 0, step_idx])
            loss_list.append(step_loss)
            p_one = gossip(p_one, cast_one) - learn_rate * g_one.astype(jnp.float32)
            p_two = gossip(p_two, cast_two) - learn_rate * g_two.astype(jnp.float32)
        return p_one[None, None], p_two[None, None], jnp.stack(loss_list)[None, None]

    grid_spec = P("tx", "ty")
    return jax.shard_map(device_train, mesh=mesh, in_specs=(grid_spec, grid_spec, grid_spec, grid_spec), out_specs=(grid_spec, grid_spec, grid_spec), check_vma=False)
```

profile of v0, /device:TPU:1, one launch (start us, length us, event | category | flops | bytes accessed | tf_op | source)
XLA Modules:
  0.0 832.8 jit_solution(822282513998403660)
XLA Ops:
  4.5 8.5 %collective-permute-start.1 = (bf16[6,128,512]{2,1,0:T(8,128)(2,1)}, bf16[6,128,512]{2,1,0:T(8,128)(2,1)}, u32[]{:S(2)}, u32[]{:S(2)}) collective-permute-start(bf16[6,128,512]{2,1,0:T(8,128)(2,1)} %bitcast_convert_fusion.1), channel_id=1, source_target_pairs={{0,63},{1,0},{2,1},{3,2},{4,3},{5,4},{6,5},{7,6},{8,7},{9,8},{10,9... | collective-permute-start | bytes 2359304 | tf_op jit(solution)/shard_map/ppermute | solution.py:58
  14.4 7.2 collective-permute-start.7
  39.3 2.8 multiply_reduce_fusion.83
  58.6 2.8 fusion.12
  73.2 4.1 fusion.867
  77.3 3.2 fusion.687
  108.1 14.3 %fusion.691 = bf16[6,512,128]{2,1,0:T(8,128)(2,1)} fusion(bf16[6,512,128]{2,1,0:T(8,128)(2,1)} %fusion.689, bf16[1024,128]{0,1:T(8,128)(2,1)S(1)} %copy-done.262, f32[1024,512]{1,0:T(8,128)S(1)} %copy-done.170), kind=kOutput, calls=%fused_computation.1175 | convolution fusion | flops 139001856 | bytes 2490368 | tf_op jit(solution)/shard_map/bf,bd->fd/dot_general | solution.py:34
  133.6 3.5 fusion.697
  137.1 3.2 fusion.1219
  140.6 7.2 collective-permute-start.4
  149.2 12.1 %collective-permute-done.6 = bf16[6,512,128]{2,1,0:T(8,128)(2,1)S(1)} collective-permute-done((bf16[6,512,128]{2,1,0:T(8,128)(2,1)}, bf16[6,512,128]{2,1,0:T(8,128)(2,1)S(1)}, u32[]{:S(2)}, u32[]{:S(2)}) %collective-permute-start.6) | collective-permute-done | bytes 786464 | tf_op jit(solution)/shard_map/ppermute | solution.py:58
  161.3 3.4 fusion.1218
  193.0 2.8 fusion.42
  206.9 4.2 fusion.865
  211.1 2.7 fusion.709
  225.7 3.4 fusion.717
  232.3 4.5 fusion.1230
  237.5 5.2 collective-permute-start.10
  244.3 10.9 %collective-permute-done.12 = bf16[6,512,128]{2,1,0:T(8,128)(2,1)S(1)} collective-permute-done((bf16[6,512,128]{2,1,0:T(8,128)(2,1)}, bf16[6,512,128]{2,1,0:T(8,128)(2,1)S(1)}, u32[]{:S(2)}, u32[]{:S(2)}) %collective-permute-start.12) | collective-permute-done | bytes 786464 | tf_op jit(solution)/shard_map/ppermute | solution.py:58
  255.2 4.2 fusion.1228
  288.3 3.0 fusion.72
  302.4 4.1 fusion.863
  306.6 3.4 fusion.731
  325.2 2.8 fusion.741
  329.8 3.4 fusion.1217
  333.9 5.3 collective-permute-start.16
  340.9 11.4 %collective-permute-done.18 = bf16[6,512,128]{2,1,0:T(8,128)(2,1)S(1)} collective-permute-done((bf16[6,512,128]{2,1,0:T(8,128)(2,1)}, bf16[6,512,128]{2,1,0:T(8,128)(2,1)S(1)}, u32[]{:S(2)}, u32[]{:S(2)}) %collective-permute-start.18) | collective-permute-done | bytes 786464 | tf_op jit(solution)/shard_map/ppermute | solution.py:58
  352.3 3.4 fusion.1216
  383.5 2.8 fusion.102
  397.5 4.2 fusion.861
  401.7 2.7 fusion.753
  420.7 4.6 fusion.1226
  425.9 5.2 collective-permute-start.22
  432.8 10.9 %collective-permute-done.24 = bf16[6,512,128]{2,1,0:T(8,128)(2,1)S(1)} collective-permute-done((bf16[6,512,128]{2,1,0:T(8,128)(2,1)}, bf16[6,512,128]{2,1,0:T(8,128)(2,1)S(1)}, u32[]{:S(2)}, u32[]{:S(2)}) %collective-permute-start.24) | collective-permute-done | bytes 786464 | tf_op jit(solution)/shard_map/ppermute | solution.py:58
  443.7 4.2 fusion.1224
  476.7 3.0 fusion.132
  490.8 4.1 fusion.859
  495.0 3.4 fusion.775
  513.6 2.8 fusion.785
  518.3 3.4 fusion.1215
  522.3 5.3 collective-permute-start.28
  529.3 11.5 %collective-permute-done.30 = bf16[6,512,128]{2,1,0:T(8,128)(2,1)S(1)} collective-permute-done((bf16[6,512,128]{2,1,0:T(8,128)(2,1)}, bf16[6,512,128]{2,1,0:T(8,128)(2,1)S(1)}, u32[]{:S(2)}, u32[]{:S(2)}) %collective-permute-start.30) | collective-permute-done | bytes 786464 | tf_op jit(solution)/shard_map/ppermute | solution.py:58
  540.8 3.5 fusion.1214
  572.4 2.8 fusion.162
  586.3 4.1 fusion.857
  605.0 3.4 fusion.805
  611.5 4.5 fusion.1222
  616.7 5.2 collective-permute-start.34
  623.5 11.0 %collective-permute-done.36 = bf16[6,512,128]{2,1,0:T(8,128)(2,1)S(1)} collective-permute-done((bf16[6,512,128]{2,1,0:T(8,128)(2,1)}, bf16[6,512,128]{2,1,0:T(8,128)(2,1)S(1)}, u32[]{:S(2)}, u32[]{:S(2)}) %collective-permute-start.36) | collective-permute-done | bytes 786464 | tf_op jit(solution)/shard_map/ppermute | solution.py:58
  634.5 4.2 fusion.1220
  667.5 3.0 fusion.192
  681.7 4.1 fusion.855
  685.8 3.4 fusion.819
  704.5 2.8 fusion.829
  709.2 3.4 fusion.1213
  713.2 5.3 collective-permute-start.40
  720.1 11.5 %collective-permute-done.42 = bf16[6,512,128]{2,1,0:T(8,128)(2,1)S(1)} collective-permute-done((bf16[6,512,128]{2,1,0:T(8,128)(2,1)}, bf16[6,512,128]{2,1,0:T(8,128)(2,1)S(1)}, u32[]{:S(2)}, u32[]{:S(2)}) %collective-permute-start.42) | collective-permute-done | bytes 786464 | tf_op jit(solution)/shard_map/ppermute | solution.py:58
  731.6 3.4 fusion.1212
  763.8 2.8 fusion.222
  777.7 4.1 fusion.853
  781.9 2.7 fusion.841
  807.8 4.9 fusion.508
  812.7 15.0 %collective-permute-done.45 = bf16[6,512,128]{2,1,0:T(8,128)(2,1)} collective-permute-done((bf16[6,512,128]{2,1,0:T(8,128)(2,1)}, bf16[6,512,128]{2,1,0:T(8,128)(2,1)}, u32[]{:S(2)}, u32[]{:S(2)}) %collective-permute-start.45) | collective-permute-done | bytes 786464 | tf_op jit(solution)/shard_map/ppermute | solution.py:58
  827.8 4.6 fusion.513
  (1189 shorter events, 496.2 us)
Async XLA Ops:
  3.2 133.9 %collective-permute-start.2 = (bf16[6,128,512]{2,1,0:T(8,128)(2,1)}, bf16[6,128,512]{2,1,0:T(8,128)(2,1)}, u32[]{:S(2)}, u32[]{:S(2)}) collective-permute-start(bf16[6,128,512]{2,1,0:T(8,128)(2,1)} %bitcast_convert_fusion.1), channel_id=1, source_target_pairs={{0,64},{64,0},{1,65},{65,1},{2,66},{66,2},{3,67},{67,3},{4,68},{68... | collective-permute-start | bytes 2359304 | tf_op jit(solution)/shard_map/ppermute | solution.py:58
  4.5 132.6 %collective-permute-start.1 = (bf16[6,128,512]{2,1,0:T(8,128)(2,1)}, bf16[6,128,512]{2,1,0:T(8,128)(2,1)}, u32[]{:S(2)}, u32[]{:S(2)}) collective-permute-start(bf16[6,128,512]{2,1,0:T(8,128)(2,1)} %bitcast_convert_fusion.1), channel_id=1, source_target_pairs={{0,63},{1,0},{2,1},{3,2},{4,3},{5,4},{6,5},{7,6},{8,7},{9,8},{10,9... | collective-permute-start | bytes 2359304 | tf_op jit(solution)/shard_map/ppermute | solution.py:58
  13.1 124.0 %collective-permute-start = (bf16[6,128,512]{2,1,0:T(8,128)(2,1)}, bf16[6,128,512]{2,1,0:T(8,128)(2,1)}, u32[]{:S(2)}, u32[]{:S(2)}) collective-permute-start(bf16[6,128,512]{2,1,0:T(8,128)(2,1)} %bitcast_convert_fusion.1), channel_id=1, source_target_pairs={{0,1},{1,2},{2,3},{3,4},{4,5},{5,6},{6,7},{7,8},{8,9},{9,10},{10,1... | collective-permute-start | bytes 2359304 | tf_op jit(solution)/shard_map/ppermute | solution.py:58
  14.1 135.0 %collective-permute-start.8 = (bf16[6,512,128]{2,1,0:T(8,128)(2,1)}, bf16[6,512,128]{2,1,0:T(8,128)(2,1)}, u32[]{:S(2)}, u32[]{:S(2)}) collective-permute-start(bf16[6,512,128]{2,1,0:T(8,128)(2,1)} %bitcast_convert_fusion), channel_id=1, source_target_pairs={{0,64},{64,0},{1,65},{65,1},{2,66},{66,2},{3,67},{67,3},{4,68},{68... | collective-permute-start | bytes 2359304 | tf_op jit(solution)/shard_map/ppermute | solution.py:58
  14.4 134.9 %collective-permute-start.7 = (bf16[6,512,128]{2,1,0:T(8,128)(2,1)}, bf16[6,512,128]{2,1,0:T(8,128)(2,1)}, u32[]{:S(2)}, u32[]{:S(2)}) collective-permute-start(bf16[6,512,128]{2,1,0:T(8,128)(2,1)} %bitcast_convert_fusion), channel_id=1, source_target_pairs={{0,63},{1,0},{2,1},{3,2},{4,3},{5,4},{6,5},{7,6},{8,7},{9,8},{10,9... | collective-permute-start | bytes 2359304 | tf_op jit(solution)/shard_map/ppermute | solution.py:58
  137.1 24.3 %collective-permute-start.6 = (bf16[6,512,128]{2,1,0:T(8,128)(2,1)}, bf16[6,512,128]{2,1,0:T(8,128)(2,1)S(1)}, u32[]{:S(2)}, u32[]{:S(2)}) collective-permute-start(bf16[6,512,128]{2,1,0:T(8,128)(2,1)} %bitcast_convert_fusion), channel_id=1, source_target_pairs={{0,1},{1,2},{2,3},{3,4},{4,5},{5,6},{6,7},{7,8},{8,9},{9,10},{10,1... | collective-permute-start | bytes 2359304 | tf_op jit(solution)/shard_map/ppermute | solution.py:58
  140.3 90.5 %collective-permute-start.5 = (bf16[6,128,512]{2,1,0:T(8,128)(2,1)}, bf16[6,128,512]{2,1,0:T(8,128)(2,1)}, u32[]{:S(2)}, u32[]{:S(2)}) collective-permute-start(bf16[6,128,512]{2,1,0:T(8,128)(2,1)} %fusion.1219), channel_id=1, source_target_pairs={{0,64},{64,0},{1,65},{65,1},{2,66},{66,2},{3,67},{67,3},{4,68},{68... | collective-permute-start | bytes 2359304 | tf_op jit(solution)/shard_map/ppermute | solution.py:58
  140.6 91.6 %collective-permute-start.4 = (bf16[6,128,512]{2,1,0:T(8,128)(2,1)}, bf16[6,128,512]{2,1,0:T(8,128)(2,1)}, u32[]{:S(2)}, u32[]{:S(2)}) collective-permute-start(bf16[6,128,512]{2,1,0:T(8,128)(2,1)} %fusion.1219), channel_id=1, source_target_pairs={{0,63},{1,0},{2,1},{3,2},{4,3},{5,4},{6,5},{7,6},{8,7},{9,8},{10,9... | collective-permute-start | bytes 2359304 | tf_op jit(solution)/shard_map/ppermute | solution.py:58
  149.1 83.1 %collective-permute-start.3 = (bf16[6,128,512]{2,1,0:T(8,128)(2,1)}, bf16[6,128,512]{2,1,0:T(8,128)(2,1)}, u32[]{:S(2)}, u32[]{:S(2)}) collective-permute-start(bf16[6,128,512]{2,1,0:T(8,128)(2,1)} %fusion.1219), channel_id=1, source_target_pairs={{0,1},{1,2},{2,3},{3,4},{4,5},{5,6},{6,7},{7,8},{8,9},{9,10},{10,1... | collective-permute-start | bytes 2359304 | tf_op jit(solution)/shard_map/ppermute | solution.py:58
  168.0 33.9 %copy-start.181 = (f32[1024,512]{1,0:T(8,128)}, f32[1024,512]{1,0:T(8,128)S(1)}, u32[]{:S(2)}) copy-start(f32[1024,512]{1,0:T(8,128)S(1)} %fusion.1089) | copy-start | bytes 6291460
  213.9 30.2 %collective-permute-start.14 = (bf16[6,512,128]{2,1,0:T(8,128)(2,1)}, bf16[6,512,128]{2,1,0:T(8,128)(2,1)}, u32[]{:S(2)}, u32[]{:S(2)}) collective-permute-start(bf16[6,512,128]{2,1,0:T(8,128)(2,1)} %fusion.1218), channel_id=1, source_target_pairs={{0,64},{64,0},{1,65},{65,1},{2,66},{66,2},{3,67},{67,3},{4,68},{68... | collective-permute-start | bytes 2359304 | tf_op jit(solution)/shard_map/ppermute | solution.py:58
  215.8 28.5 %collective-permute-start.13 = (bf16[6,512,128]{2,1,0:T(8,128)(2,1)}, bf16[6,512,128]{2,1,0:T(8,128)(2,1)}, u32[]{:S(2)}, u32[]{:S(2)}) collective-permute-start(bf16[6,512,128]{2,1,0:T(8,128)(2,1)} %fusion.1218), channel_id=1, source_target_pairs={{0,63},{1,0},{2,1},{3,2},{4,3},{5,4},{6,5},{7,6},{8,7},{9,8},{10,9... | collective-permute-start | bytes 2359304 | tf_op jit(solution)/shard_map/ppermute | solution.py:58
  230.8 24.4 %collective-permute-start.12 = (bf16[6,512,128]{2,1,0:T(8,128)(2,1)}, bf16[6,512,128]{2,1,0:T(8,128)(2,1)S(1)}, u32[]{:S(2)}, u32[]{:S(2)}) collective-permute-start(bf16[6,512,128]{2,1,0:T(8,128)(2,1)} %fusion.1218), channel_id=1, source_target_pairs={{0,1},{1,2},{2,3},{3,4},{4,5},{5,6},{6,7},{7,8},{8,9},{9,10},{10,1... | collective-permute-start | bytes 2359304 | tf_op jit(solution)/shard_map/ppermute | solution.py:58
  236.8 93.0 %copy-start.4 = (f32[6,128,512]{2,1,0:T(8,128)}, f32[6,128,512]{2,1,0:T(8,128)S(1)}, u32[]{:S(2)}) copy-start(f32[6,128,512]{2,1,0:T(8,128)S(1)} %get-tuple-element.14) | copy-start | bytes 4718596
  236.8 91.2 %collective-permute-start.11 = (bf16[6,128,512]{2,1,0:T(8,128)(2,1)}, bf16[6,128,512]{2,1,0:T(8,128)(2,1)}, u32[]{:S(2)}, u32[]{:S(2)}) collective-permute-start(bf16[6,128,512]{2,1,0:T(8,128)(2,1)} %get-tuple-element.13), channel_id=1, source_target_pairs={{0,64},{64,0},{1,65},{65,1},{2,66},{66,2},{3,67},{67,3},{4,68},{68... | collective-permute-start | bytes 2359304 | tf_op jit(solution)/shard_map/ppermute | solution.py:58
  237.5 92.2 %collective-permute-start.10 = (bf16[6,128,512]{2,1,0:T(8,128)(2,1)}, bf16[6,128,512]{2,1,0:T(8,128)(2,1)}, u32[]{:S(2)}, u32[]{:S(2)}) collective-permute-start(bf16[6,128,512]{2,1,0:T(8,128)(2,1)} %get-tuple-element.13), channel_id=1, source_target_pairs={{0,63},{1,0},{2,1},{3,2},{4,3},{5,4},{6,5},{7,6},{8,7},{9,8},{10,9... | collective-permute-start | bytes 2359304 | tf_op jit(solution)/shard_map/ppermute | solution.py:58
  244.1 85.7 %collective-permute-start.9 = (bf16[6,128,512]{2,1,0:T(8,128)(2,1)}, bf16[6,128,512]{2,1,0:T(8,128)(2,1)}, u32[]{:S(2)}, u32[]{:S(2)}) collective-permute-start(bf16[6,128,512]{2,1,0:T(8,128)(2,1)} %get-tuple-element.13), channel_id=1, source_target_pairs={{0,1},{1,2},{2,3},{3,4},{4,5},{5,6},{6,7},{7,8},{8,9},{9,10},{10,1... | collective-permute-start | bytes 2359304 | tf_op jit(solution)/shard_map/ppermute | solution.py:58
  259.4 92.9 %copy-start.2 = (f32[6,512,128]{2,1,0:T(8,128)}, f32[6,512,128]{2,1,0:T(8,128)S(1)}, u32[]{:S(2)}) copy-start(f32[6,512,128]{2,1,0:T(8,128)S(1)} %get-tuple-element.12) | copy-start | bytes 4718596
  261.3 40.2 %copy-start.20 = (f32[1024,128]{0,1:T(8,128)}, f32[1024,128]{0,1:T(8,128)S(1)}, u32[]{:S(2)}) copy-start(f32[1024,128]{0,1:T(8,128)S(1)} %get-tuple-element.88) | copy-start | bytes 1572868
  262.9 34.5 %copy-start.213 = (f32[1024,512]{1,0:T(8,128)}, f32[1024,512]{1,0:T(8,128)S(1)}, u32[]{:S(2)}) copy-start(f32[1024,512]{1,0:T(8,128)S(1)} %fusion.1094) | copy-start | bytes 6291460
  264.8 32.4 %copy-start.28 = (f32[1024,128]{0,1:T(8,128)}, f32[1024,128]{0,1:T(8,128)S(1)}, u32[]{:S(2)}) copy-start(f32[1024,128]{0,1:T(8,128)S(1)} %get-tuple-element.90) | copy-start | bytes 1572868
  309.9 30.6 %collective-permute-start.20 = (bf16[6,512,128]{2,1,0:T(8,128)(2,1)}, bf16[6,512,128]{2,1,0:T(8,128)(2,1)}, u32[]{:S(2)}, u32[]{:S(2)}) collective-permute-start(bf16[6,512,128]{2,1,0:T(8,128)(2,1)} %get-tuple-element.11), channel_id=1, source_target_pairs={{0,64},{64,0},{1,65},{65,1},{2,66},{66,2},{3,67},{67,3},{4,68},{68... | collective-permute-start | bytes 2359304 | tf_op jit(solution)/shard_map/ppermute | solution.py:58
  311.4 29.4 %collective-permute-start.19 = (bf16[6,512,128]{2,1,0:T(8,128)(2,1)}, bf16[6,512,128]{2,1,0:T(8,128)(2,1)}, u32[]{:S(2)}, u32[]{:S(2)}) collective-permute-start(bf16[6,512,128]{2,1,0:T(8,128)(2,1)} %get-tuple-element.11), channel_id=1, source_target_pairs={{0,63},{1,0},{2,1},{3,2},{4,3},{5,4},{6,5},{7,6},{8,7},{9,8},{10,9... | collective-permute-start | bytes 2359304 | tf_op jit(solution)/shard_map/ppermute | solution.py:58
  328.0 24.3 %collective-permute-start.18 = (bf16[6,512,128]{2,1,0:T(8,128)(2,1)}, bf16[6,512,128]{2,1,0:T(8,128)(2,1)S(1)}, u32[]{:S(2)}, u32[]{:S(2)}) collective-permute-start(bf16[6,512,128]{2,1,0:T(8,128)(2,1)} %get-tuple-element.11), channel_id=1, source_target_pairs={{0,1},{1,2},{2,3},{3,4},{4,5},{5,6},{6,7},{7,8},{8,9},{9,10},{10,1... | collective-permute-start | bytes 2359304 | tf_op jit(solution)/shard_map/ppermute | solution.py:58
  333.2 86.0 %collective-permute-start.17 = (bf16[6,128,512]{2,1,0:T(8,128)(2,1)}, bf16[6,128,512]{2,1,0:T(8,128)(2,1)}, u32[]{:S(2)}, u32[]{:S(2)}) collective-permute-start(bf16[6,128,512]{2,1,0:T(8,128)(2,1)} %fusion.1217), channel_id=1, source_target_pairs={{0,64},{64,0},{1,65},{65,1},{2,66},{66,2},{3,67},{67,3},{4,68},{68... | collective-permute-start | bytes 2359304 | tf_op jit(solution)/shard_map/ppermute | solution.py:58
  333.9 86.8 %collective-permute-start.16 = (bf16[6,128,512]{2,1,0:T(8,128)(2,1)}, bf16[6,128,512]{2,1,0:T(8,128)(2,1)}, u32[]{:S(2)}, u32[]{:S(2)}) collective-permute-start(bf16[6,128,512]{2,1,0:T(8,128)(2,1)} %fusion.1217), channel_id=1, source_target_pairs={{0,63},{1,0},{2,1},{3,2},{4,3},{5,4},{6,5},{7,6},{8,7},{9,8},{10,9... | collective-permute-start | bytes 2359304 | tf_op jit(solution)/shard_map/ppermute | solution.py:58
  340.6 80.1 %collective-permute-start.15 = (bf16[6,128,512]{2,1,0:T(8,128)(2,1)}, bf16[6,128,512]{2,1,0:T(8,128)(2,1)}, u32[]{:S(2)}, u32[]{:S(2)}) collective-permute-start(bf16[6,128,512]{2,1,0:T(8,128)(2,1)} %fusion.1217), channel_id=1, source_target_pairs={{0,1},{1,2},{2,3},{3,4},{4,5},{5,6},{6,7},{7,8},{8,9},{9,10},{10,1... | collective-permute-start | bytes 2359304 | tf_op jit(solution)/shard_map/ppermute | solution.py:58
  358.9 33.5 %copy-start.185 = (f32[1024,512]{1,0:T(8,128)}, f32[1024,512]{1,0:T(8,128)S(1)}, u32[]{:S(2)}) copy-start(f32[1024,512]{1,0:T(8,128)S(1)} %fusion.1099) | copy-start | bytes 6291460
  404.4 28.1 %collective-permute-start.26 = (bf16[6,512,128]{2,1,0:T(8,128)(2,1)}, bf16[6,512,128]{2,1,0:T(8,128)(2,1)}, u32[]{:S(2)}, u32[]{:S(2)}) collective-permute-start(bf16[6,512,128]{2,1,0:T(8,128)(2,1)} %fusion.1216), channel_id=1, source_target_pairs={{0,64},{64,0},{1,65},{65,1},{2,66},{66,2},{3,67},{67,3},{4,68},{68... | collective-permute-start | bytes 2359304 | tf_op jit(solution)/shard_map/ppermute | solution.py:58
  406.2 26.5 %collective-permute-start.25 = (bf16[6,512,128]{2,1,0:T(8,128)(2,1)}, bf16[6,512,128]{2,1,0:T(8,128)(2,1)}, u32[]{:S(2)}, u32[]{:S(2)}) collective-permute-start(bf16[6,512,128]{2,1,0:T(8,128)(2,1)} %fusion.1216), channel_id=1, source_target_pairs={{0,63},{1,0},{2,1},{3,2},{4,3},{5,4},{6,5},{7,6},{8,7},{9,8},{10,9... | collective-permute-start | bytes 2359304 | tf_op jit(solution)/shard_map/ppermute | solution.py:58
  419.2 24.4 %collective-permute-start.24 = (bf16[6,512,128]{2,1,0:T(8,128)(2,1)}, bf16[6,512,128]{2,1,0:T(8,128)(2,1)S(1)}, u32[]{:S(2)}, u32[]{:S(2)}) collective-permute-start(bf16[6,512,128]{2,1,0:T(8,128)(2,1)} %fusion.1216), channel_id=1, source_target_pairs={{0,1},{1,2},{2,3},{3,4},{4,5},{5,6},{6,7},{7,8},{8,9},{9,10},{10,1... | collective-permute-start | bytes 2359304 | tf_op jit(solution)/shard_map/ppermute | solution.py:58
  425.3 91.2 %collective-permute-start.23 = (bf16[6,128,512]{2,1,0:T(8,128)(2,1)}, bf16[6,128,512]{2,1,0:T(8,128)(2,1)}, u32[]{:S(2)}, u32[]{:S(2)}) collective-permute-start(bf16[6,128,512]{2,1,0:T(8,128)(2,1)} %get-tuple-element.9), channel_id=1, source_target_pairs={{0,64},{64,0},{1,65},{65,1},{2,66},{66,2},{3,67},{67,3},{4,68},{68... | collective-permute-start | bytes 2359304 | tf_op jit(solution)/shard_map/ppermute | solution.py:58
  425.9 92.3 %collective-permute-start.22 = (bf16[6,128,512]{2,1,0:T(8,128)(2,1)}, bf16[6,128,512]{2,1,0:T(8,128)(2,1)}, u32[]{:S(2)}, u32[]{:S(2)}) collective-permute-start(bf16[6,128,512]{2,1,0:T(8,128)(2,1)} %get-tuple-element.9), channel_id=1, source_target_pairs={{0,63},{1,0},{2,1},{3,2},{4,3},{5,4},{6,5},{7,6},{8,7},{9,8},{10,9... | collective-permute-start | bytes 2359304 | tf_op jit(solution)/shard_map/ppermute | solution.py:58
  432.5 85.7 %collective-permute-start.21 = (bf16[6,128,512]{2,1,0:T(8,128)(2,1)}, bf16[6,128,512]{2,1,0:T(8,128)(2,1)}, u32[]{:S(2)}, u32[]{:S(2)}) collective-permute-start(bf16[6,128,512]{2,1,0:T(8,128)(2,1)} %get-tuple-element.9), channel_id=1, source_target_pairs={{0,1},{1,2},{2,3},{3,4},{4,5},{5,6},{6,7},{7,8},{8,9},{9,10},{10,1... | collective-permute-start | bytes 2359304 | tf_op jit(solution)/shard_map/ppermute | solution.py:58
  447.8 92.9 %copy-start = (f32[6,512,128]{2,1,0:T(8,128)}, f32[6,512,128]{2,1,0:T(8,128)S(1)}, u32[]{:S(2)}) copy-start(f32[6,512,128]{2,1,0:T(8,128)S(1)} %get-tuple-element.8) | copy-start | bytes 4718596
  449.7 40.2 %copy-start.22 = (f32[1024,128]{0,1:T(8,128)}, f32[1024,128]{0,1:T(8,128)S(1)}, u32[]{:S(2)}) copy-start(f32[1024,128]{0,1:T(8,128)S(1)} %get-tuple-element.128) | copy-start | bytes 1572868
  451.3 34.5 %copy-start.215 = (f32[1024,512]{1,0:T(8,128)}, f32[1024,512]{1,0:T(8,128)S(1)}, u32[]{:S(2)}) copy-start(f32[1024,512]{1,0:T(8,128)S(1)} %fusion.1104) | copy-start | bytes 6291460
  453.2 32.4 %copy-start.30 = (f32[1024,128]{0,1:T(8,128)}, f32[1024,128]{0,1:T(8,128)S(1)}, u32[]{:S(2)}) copy-start(f32[1024,128]{0,1:T(8,128)S(1)} %get-tuple-element.130) | copy-start | bytes 1572868
  498.3 30.7 %collective-permute-start.32 = (bf16[6,512,128]{2,1,0:T(8,128)(2,1)}, bf16[6,512,128]{2,1,0:T(8,128)(2,1)}, u32[]{:S(2)}, u32[]{:S(2)}) collective-permute-start(bf16[6,512,128]{2,1,0:T(8,128)(2,1)} %get-tuple-element.7), channel_id=1, source_target_pairs={{0,64},{64,0},{1,65},{65,1},{2,66},{66,2},{3,67},{67,3},{4,68},{68... | collective-permute-start | bytes 2359304 | tf_op jit(solution)/shard_map/ppermute | solution.py:58
  499.9 29.4 %collective-permute-start.31 = (bf16[6,512,128]{2,1,0:T(8,128)(2,1)}, bf16[6,512,128]{2,1,0:T(8,128)(2,1)}, u32[]{:S(2)}, u32[]{:S(2)}) collective-permute-start(bf16[6,512,128]{2,1,0:T(8,128)(2,1)} %get-tuple-element.7), channel_id=1, source_target_pairs={{0,63},{1,0},{2,1},{3,2},{4,3},{5,4},{6,5},{7,6},{8,7},{9,8},{10,9... | collective-permute-start | bytes 2359304 | tf_op jit(solution)/shard_map/ppermute | solution.py:58
  516.4 24.3 %collective-permute-start.30 = (bf16[6,512,128]{2,1,0:T(8,128)(2,1)}, bf16[6,512,128]{2,1,0:T(8,128)(2,1)S(1)}, u32[]{:S(2)}, u32[]{:S(2)}) collective-permute-start(bf16[6,512,128]{2,1,0:T(8,128)(2,1)} %get-tuple-element.7), channel_id=1, source_target_pairs={{0,1},{1,2},{2,3},{3,4},{4,5},{5,6},{6,7},{7,8},{8,9},{9,10},{10,1... | collective-permute-start | bytes 2359304 | tf_op jit(solution)/shard_map/ppermute | solution.py:58
  521.7 88.4 %collective-permute-start.29 = (bf16[6,128,512]{2,1,0:T(8,128)(2,1)}, bf16[6,128,512]{2,1,0:T(8,128)(2,1)}, u32[]{:S(2)}, u32[]{:S(2)}) collective-permute-start(bf16[6,128,512]{2,1,0:T(8,128)(2,1)} %fusion.1215), channel_id=1, source_target_pairs={{0,64},{64,0},{1,65},{65,1},{2,66},{66,2},{3,67},{67,3},{4,68},{68... | collective-permute-start | bytes 2359304 | tf_op jit(solution)/shard_map/ppermute | solution.py:58
  522.3 89.2 %collective-permute-start.28 = (bf16[6,128,512]{2,1,0:T(8,128)(2,1)}, bf16[6,128,512]{2,1,0:T(8,128)(2,1)}, u32[]{:S(2)}, u32[]{:S(2)}) collective-permute-start(bf16[6,128,512]{2,1,0:T(8,128)(2,1)} %fusion.1215), channel_id=1, source_target_pairs={{0,63},{1,0},{2,1},{3,2},{4,3},{5,4},{6,5},{7,6},{8,7},{9,8},{10,9... | collective-permute-start | bytes 2359304 | tf_op jit(solution)/shard_map/ppermute | solution.py:58
  529.0 82.5 %collective-permute-start.27 = (bf16[6,128,512]{2,1,0:T(8,128)(2,1)}, bf16[6,128,512]{2,1,0:T(8,128)(2,1)}, u32[]{:S(2)}, u32[]{:S(2)}) collective-permute-start(bf16[6,128,512]{2,1,0:T(8,128)(2,1)} %fusion.1215), channel_id=1, source_target_pairs={{0,1},{1,2},{2,3},{3,4},{4,5},{5,6},{6,7},{7,8},{8,9},{9,10},{10,1... | collective-permute-start | bytes 2359304 | tf_op jit(solution)/shard_map/ppermute | solution.py:58
  547.4 33.9 %copy-start.189 = (f32[1024,512]{1,0:T(8,128)}, f32[1024,512]{1,0:T(8,128)S(1)}, u32[]{:S(2)}) copy-start(f32[1024,512]{1,0:T(8,128)S(1)} %fusion.1109) | copy-start | bytes 6291460
  593.2 30.0 %collective-permute-start.38 = (bf16[6,512,128]{2,1,0:T(8,128)(2,1)}, bf16[6,512,128]{2,1,0:T(8,128)(2,1)}, u32[]{:S(2)}, u32[]{:S(2)}) collective-permute-start(bf16[6,512,128]{2,1,0:T(8,128)(2,1)} %fusion.1214), channel_id=1, source_target_pairs={{0,64},{64,0},{1,65},{65,1},{2,66},{66,2},{3,67},{67,3},{4,68},{68... | collective-permute-start | bytes 2359304 | tf_op jit(solution)/shard_map/ppermute | solution.py:58
  595.0 28.5 %collective-permute-start.37 = (bf16[6,512,128]{2,1,0:T(8,128)(2,1)}, bf16[6,512,128]{2,1,0:T(8,128)(2,1)}, u32[]{:S(2)}, u32[]{:S(2)}) collective-permute-start(bf16[6,512,128]{2,1,0:T(8,128)(2,1)} %fusion.1214), channel_id=1, source_target_pairs={{0,63},{1,0},{2,1},{3,2},{4,3},{5,4},{6,5},{7,6},{8,7},{9,8},{10,9... | collective-permute-start | bytes 2359304 | tf_op jit(solution)/shard_map/ppermute | solution.py:58
  610.1 24.4 %collective-permute-start.36 = (bf16[6,512,128]{2,1,0:T(8,128)(2,1)}, bf16[6,512,128]{2,1,0:T(8,128)(2,1)S(1)}, u32[]{:S(2)}, u32[]{:S(2)}) collective-permute-start(bf16[6,512,128]{2,1,0:T(8,128)(2,1)} %fusion.1214), channel_id=1, source_target_pairs={{0,1},{1,2},{2,3},{3,4},{4,5},{5,6},{6,7},{7,8},{8,9},{9,10},{10,1... | collective-permute-start | bytes 2359304 | tf_op jit(solution)/shard_map/ppermute | solution.py:58
  616.0 91.3 %collective-permute-start.35 = (bf16[6,128,512]{2,1,0:T(8,128)(2,1)}, bf16[6,128,512]{2,1,0:T(8,128)(2,1)}, u32[]{:S(2)}, u32[]{:S(2)}) collective-permute-start(bf16[6,128,512]{2,1,0:T(8,128)(2,1)} %get-tuple-element.5), channel_id=1, source_target_pairs={{0,64},{64,0},{1,65},{65,1},{2,66},{66,2},{3,67},{67,3},{4,68},{68... | collective-permute-start | bytes 2359304 | tf_op jit(solution)/shard_map/ppermute | solution.py:58
  616.7 92.4 %collective-permute-start.34 = (bf16[6,128,512]{2,1,0:T(8,128)(2,1)}, bf16[6,128,512]{2,1,0:T(8,128)(2,1)}, u32[]{:S(2)}, u32[]{:S(2)}) collective-permute-start(bf16[6,128,512]{2,1,0:T(8,128)(2,1)} %get-tuple-element.5), channel_id=1, source_target_pairs={{0,63},{1,0},{2,1},{3,2},{4,3},{5,4},{6,5},{7,6},{8,7},{9,8},{10,9... | collective-permute-start | bytes 2359304 | tf_op jit(solution)/shard_map/ppermute | solution.py:58
  623.2 85.9 %collective-permute-start.33 = (bf16[6,128,512]{2,1,0:T(8,128)(2,1)}, bf16[6,128,512]{2,1,0:T(8,128)(2,1)}, u32[]{:S(2)}, u32[]{:S(2)}) collective-permute-start(bf16[6,128,512]{2,1,0:T(8,128)(2,1)} %get-tuple-element.5), channel_id=1, source_target_pairs={{0,1},{1,2},{2,3},{3,4},{4,5},{5,6},{6,7},{7,8},{8,9},{9,10},{10,1... | collective-permute-start | bytes 2359304 | tf_op jit(solution)/shard_map/ppermute | solution.py:58
  640.6 40.2 %copy-start.24 = (f32[1024,128]{0,1:T(8,128)}, f32[1024,128]{0,1:T(8,128)S(1)}, u32[]{:S(2)}) copy-start(f32[1024,128]{0,1:T(8,128)S(1)} %get-tuple-element.168) | copy-start | bytes 1572868
  642.1 34.5 %copy-start.217 = (f32[1024,512]{1,0:T(8,128)}, f32[1024,512]{1,0:T(8,128)S(1)}, u32[]{:S(2)}) copy-start(f32[1024,512]{1,0:T(8,128)S(1)} %fusion.1114) | copy-start | bytes 6291460
  689.2 30.6 %collective-permute-start.44 = (bf16[6,512,128]{2,1,0:T(8,128)(2,1)}, bf16[6,512,128]{2,1,0:T(8,128)(2,1)}, u32[]{:S(2)}, u32[]{:S(2)}) collective-permute-start(bf16[6,512,128]{2,1,0:T(8,128)(2,1)} %get-tuple-element.3), channel_id=1, source_target_pairs={{0,64},{64,0},{1,65},{65,1},{2,66},{66,2},{3,67},{67,3},{4,68},{68... | collective-permute-start | bytes 2359304 | tf_op jit(solution)/shard_map/ppermute | solution.py:58
  690.7 29.4 %collective-permute-start.43 = (bf16[6,512,128]{2,1,0:T(8,128)(2,1)}, bf16[6,512,128]{2,1,0:T(8,128)(2,1)}, u32[]{:S(2)}, u32[]{:S(2)}) collective-permute-start(bf16[6,512,128]{2,1,0:T(8,128)(2,1)} %get-tuple-element.3), channel_id=1, source_target_pairs={{0,63},{1,0},{2,1},{3,2},{4,3},{5,4},{6,5},{7,6},{8,7},{9,8},{10,9... | collective-permute-start | bytes 2359304 | tf_op jit(solution)/shard_map/ppermute | solution.py:58
  707.3 24.3 %collective-permute-start.42 = (bf16[6,512,128]{2,1,0:T(8,128)(2,1)}, bf16[6,512,128]{2,1,0:T(8,128)(2,1)S(1)}, u32[]{:S(2)}, u32[]{:S(2)}) collective-permute-start(bf16[6,512,128]{2,1,0:T(8,128)(2,1)} %get-tuple-element.3), channel_id=1, source_target_pairs={{0,1},{1,2},{2,3},{3,4},{4,5},{5,6},{6,7},{7,8},{8,9},{9,10},{10,1... | collective-permute-start | bytes 2359304 | tf_op jit(solution)/shard_map/ppermute | solution.py:58
  712.5 90.7 %collective-permute-start.41 = (bf16[6,128,512]{2,1,0:T(8,128)(2,1)}, bf16[6,128,512]{2,1,0:T(8,128)(2,1)}, u32[]{:S(2)}, u32[]{:S(2)}) collective-permute-start(bf16[6,128,512]{2,1,0:T(8,128)(2,1)} %fusion.1213), channel_id=1, source_target_pairs={{0,64},{64,0},{1,65},{65,1},{2,66},{66,2},{3,67},{67,3},{4,68},{68... | collective-permute-start | bytes 2359304 | tf_op jit(solution)/shard_map/ppermute | solution.py:58
  713.2 94.5 %collective-permute-start.40 = (bf16[6,128,512]{2,1,0:T(8,128)(2,1)}, bf16[6,128,512]{2,1,0:T(8,128)(2,1)}, u32[]{:S(2)}, u32[]{:S(2)}) collective-permute-start(bf16[6,128,512]{2,1,0:T(8,128)(2,1)} %fusion.1213), channel_id=1, source_target_pairs={{0,63},{1,0},{2,1},{3,2},{4,3},{5,4},{6,5},{7,6},{8,7},{9,8},{10,9... | collective-permute-start | bytes 2359304 | tf_op jit(solution)/shard_map/ppermute | solution.py:58
  719.9 87.9 %collective-permute-start.39 = (bf16[6,128,512]{2,1,0:T(8,128)(2,1)}, bf16[6,128,512]{2,1,0:T(8,128)(2,1)}, u32[]{:S(2)}, u32[]{:S(2)}) collective-permute-start(bf16[6,128,512]{2,1,0:T(8,128)(2,1)} %fusion.1213), channel_id=1, source_target_pairs={{0,1},{1,2},{2,3},{3,4},{4,5},{5,6},{6,7},{7,8},{8,9},{9,10},{10,1... | collective-permute-start | bytes 2359304 | tf_op jit(solution)/shard_map/ppermute | solution.py:58
  736.8 40.1 %copy-start.26 = (f32[1024,128]{0,1:T(8,128)}, f32[1024,128]{0,1:T(8,128)S(1)}, u32[]{:S(2)}) copy-start(f32[1024,128]{0,1:T(8,128)S(1)} %get-tuple-element.188) | copy-start | bytes 1572868
  738.4 34.3 %copy-start.219 = (f32[1024,512]{1,0:T(8,128)}, f32[1024,512]{1,0:T(8,128)S(1)}, u32[]{:S(2)}) copy-start(f32[1024,512]{1,0:T(8,128)S(1)} %fusion.1119) | copy-start | bytes 6291460
  784.6 28.1 %collective-permute-start.47 = (bf16[6,512,128]{2,1,0:T(8,128)(2,1)}, bf16[6,512,128]{2,1,0:T(8,128)(2,1)}, u32[]{:S(2)}, u32[]{:S(2)}) collective-permute-start(bf16[6,512,128]{2,1,0:T(8,128)(2,1)} %fusion.1212), channel_id=1, source_target_pairs={{0,64},{64,0},{1,65},{65,1},{2,66},{66,2},{3,67},{67,3},{4,68},{68... | collective-permute-start | bytes 2359304 | tf_op jit(solution)/shard_map/ppermute | solution.py:58
  786.5 26.2 %collective-permute-start.46 = (bf16[6,512,128]{2,1,0:T(8,128)(2,1)}, bf16[6,512,128]{2,1,0:T(8,128)(2,1)}, u32[]{:S(2)}, u32[]{:S(2)}) collective-permute-start(bf16[6,512,128]{2,1,0:T(8,128)(2,1)} %fusion.1212), channel_id=1, source_target_pairs={{0,63},{1,0},{2,1},{3,2},{4,3},{5,4},{6,5},{7,6},{8,7},{9,8},{10,9... | collective-permute-start | bytes 2359304 | tf_op jit(solution)/shard_map/ppermute | solution.py:58
  803.2 24.5 %collective-permute-start.45 = (bf16[6,512,128]{2,1,0:T(8,128)(2,1)}, bf16[6,512,128]{2,1,0:T(8,128)(2,1)}, u32[]{:S(2)}, u32[]{:S(2)}) collective-permute-start(bf16[6,512,128]{2,1,0:T(8,128)(2,1)} %fusion.1212), channel_id=1, source_target_pairs={{0,1},{1,2},{2,3},{3,4},{4,5},{5,6},{6,7},{7,8},{8,9},{9,10},{10,1... | collective-permute-start | bytes 2359304 | tf_op jit(solution)/shard_map/ppermute | solution.py:58
  (340 other events, 2049.0 us)
where the time goes:
time: 849 us; the launch traced here: 833 us
  matrix products  510 us (60%)
  waiting for transfers between devices  94.4 us (11%)
  other arithmetic  90 us (11%)
  starting transfers between devices  85.3 us (10%)
  local copies, waits for them, and re-layouts  41.8 us (5%)
  between operations  11.8 us (1%)
    dot_general x40, matrix products, local_grads(): jnp.einsum('bd,fd->bf', d_hidden, cast_two[layer_idx], preferred_element_...  106 us
    dot_general x48, matrix products, local_grads(): jnp.einsum('bf,bd->fd', hidden_act, d_hidden, preferred_element_type=jnp....  104 us
    ppermute x48, waiting for transfers between devices, gossip(): lax.ppermute(cast_copy, axis_name, perm_pairs)  94.4 us
    dot_general x48, matrix products, local_grads(): jnp.dot(hidden_act, cast_two[layer_idx], preferred_element_type=jnp.float32)  92.9 us
    ppermute x48, starting transfers between devices, gossip(): lax.ppermute(cast_copy, axis_name, perm_pairs)  85.3 us
    dot_general x48, matrix products, local_grads(): jnp.einsum('bd,bf->df', normed, d_pre_b, preferred_element_type=jnp.float32)  74.6 us
    dot_general x48, matrix products, local_grads(): jnp.dot(normed, cast_one[layer_idx], preferred_element_type=jnp.float32)  70 us
    dot_general x40, matrix products, local_grads(): jnp.einsum('bf,df->bd', d_pre_b, cast_one[layer_idx], preferred_element_t...  61.9 us
  transfers between devices with their start and end apart: 48, of which 8 were waited for; matrix products, arithmetic and copies ran while one was open for 74% of the time, Pallas kernels for 0%

commit v1 on v0

v1 whole, which is shorter than its diff:
```python
import functools

import jax
import jax.numpy as jnp
from jax import lax
from jax.experimental import pallas as pl
from jax.experimental.pallas import tpu as pltpu
from jax.sharding import PartitionSpec as P

NORM_EPS = 1e-6
GELU_SCALE = 0.7978845608028654
GELU_CUBIC = 0.044715
MESH = pl.DeviceIdType.MESH
BF16 = jnp.bfloat16
F32 = jnp.float32


def dot(lhs, rhs, lhs_dim, rhs_dim):
    return lax.dot_general(lhs, rhs, (((lhs_dim,), (rhs_dim,)), ((), ())), preferred_element_type=F32)


def train_kernel(
    dims,
    w_one, w_two, inputs, targets,
    out_one, out_two, losses,
    master, copies, recv, hidden, normed, inv_rms, act, slope, d_hid, d_pre, goals, stage,
    load_sem, data_sem, send_sem, recv_sem, out_sem,
):
    grid_x, steps, layers, rows, width, ffn, block = dims
    learn_rate = width / (ffn * layers)
    blocks = [pl.ds(start, block) for start in range(0, rows, block)]
    me_x = lax.axis_index("tx")
    me_y = lax.axis_index("ty")
    next_x = lax.rem(me_x + 1, grid_x)
    prev_x = lax.rem(me_x + grid_x - 1, grid_x)
    peers = ({"tx": next_x}, {"tx": prev_x}, {"ty": 1 - me_y})

    def load_copies(layer):
        return (
            pltpu.make_async_copy(w_one.at[layer], master.at[layer, pl.ds(0, width)], load_sem.at[0, layer]),
            pltpu.make_async_copy(w_two.at[layer], stage.at[layer], load_sem.at[1, layer]),
        )

    def out_copies(layer):
        return (
            pltpu.make_async_copy(master.at[layer, pl.ds(0, width)], out_one.at[layer], out_sem.at[0, layer]),
            pltpu.make_async_copy(stage.at[layer], out_two.at[layer], out_sem.at[1, layer]),
        )

    def acts_copy(step):
        return pltpu.make_async_copy(inputs.at[step], hidden.at[0], data_sem.at[0])

    def goals_copy(step):
        return pltpu.make_async_copy(targets.at[step], goals, data_sem.at[1])

    def sends(slot, layer):
        return [
            pltpu.make_async_remote_copy(
                src_ref=copies.at[slot, layer],
                dst_ref=recv.at[peer_idx, slot, layer],
                send_sem=send_sem.at[peer_idx, slot, layer],
                recv_sem=recv_sem.at[peer_idx, slot, layer],
                device_id=peer,
                device_id_type=MESH,
            )
            for peer_idx, peer in enumerate(peers)
        ]

    for layer in reversed(range(layers)):
        for copy in load_copies(layer):
            copy.start()
    acts_copy(0).start()
    goals_copy(0).start()

    barrier = pltpu.get_barrier_semaphore()
    for peer in peers:
        pl.semaphore_signal(barrier, inc=1, device_id=peer, device_id_type=MESH)
    pl.semaphore_wait(barrier, 3)

    def first_body(idx, carry):
        layer = layers - 1 - idx
        for copy in load_copies(layer):
            copy.wait()
        copies[0, layer, :width, :] = master[layer, :width, :].astype(BF16)
        turned = stage[layer].T
        master[layer, width:, :] = turned
        copies[0, layer, width:, :] = turned.astype(BF16)
        for copy in sends(0, layer):
            copy.start()
        return carry

    lax.fori_loop(0, layers, first_body, 0)

    def step_body(step, carry):
        slot = lax.rem(step, 2)
        later = 1 - slot
        acts_copy(step).wait()

        def forward_body(layer, inner):
            cast_one = copies[slot, layer, :width, :]
            cast_two = copies[slot, layer, width:, :]
            for rows_ds in blocks:
                hid_f = hidden[layer, rows_ds, :].astype(F32)
                inv = lax.rsqrt(jnp.mean(hid_f * hid_f, axis=-1, keepdims=True) + NORM_EPS)
                inv = jnp.broadcast_to(inv, hid_f.shape)
                normed_b = (hid_f * inv).astype(BF16)
                inv_rms[layer, rows_ds, :] = inv
                normed[layer, rows_ds, :] = normed_b
                pre = dot(normed_b, cast_one, 1, 0)
                square = pre * pre
                tanh_v = jnp.tanh(pre * (GELU_SCALE + (GELU_SCALE * GELU_CUBIC) * square))
                cdf = 0.5 + 0.5 * tanh_v
                act_b = (pre * cdf).astype(BF16)
                act[layer, rows_ds, :] = act_b
                inner_slope = 0.5 * GELU_SCALE + (1.5 * GELU_SCALE * GELU_CUBIC) * square
                slope[layer, rows_ds, :] = cdf + (pre * inner_slope) * (1.0 - tanh_v * tanh_v)
                mlp_out = dot(act_b, cast_two, 1, 1)
                hidden[layer + 1, rows_ds, :] = (hid_f + mlp_out).astype(BF16)
            return inner

        lax.fori_loop(0, layers, forward_body, 0)

        @pl.when(step + 1 < steps)
        def _():
            acts_copy(step + 1).start()

        goals_copy(step).wait()
        total = jnp.zeros((8, width), F32)
        for rows_ds in blocks:
            error_term = hidden[layers, rows_ds, :].astype(F32) - goals[rows_ds, :].astype(F32)
            d_hid[rows_ds, :] = (error_term * (2.0 / (rows * width))).astype(BF16)
            total = total + jnp.sum((error_term * error_term).reshape(block // 8, 8, width), axis=0)
        losses[step] = jnp.sum(total) / (rows * width)

        @pl.when(step + 1 < steps)
        def _():
            goals_copy(step + 1).start()

        def backward_body(idx, inner):
            layer = layers - 1 - idx
            cast_two = copies[slot, layer, width:, :]
            for rows_ds in blocks:
                d_act = dot(d_hid[rows_ds, :], cast_two, 1, 0).astype(BF16).astype(F32)
                d_pre[rows_ds, :] = (d_act * slope[layer, rows_ds, :]).astype(BF16)
            grad_two = dot(d_hid[...], act[layer], 0, 0).astype(BF16)
            grad_one = dot(normed[layer], d_pre[...], 0, 0).astype(BF16)

            for copy in sends(slot, layer):
                copy.wait_recv()

            @pl.when(step > 0)
            def _():
                for copy in sends(later, layer):
                    copy.wait_send()

            for start, grad in ((0, grad_one), (width, grad_two)):
                part = pl.ds(start, width)
                other = recv[2, slot, layer, part, :].astype(F32)
                mixed = master[layer, part, :] + recv[0, slot, layer, part, :].astype(F32)
                mixed = mixed + recv[1, slot, layer, part, :].astype(F32)
                mixed = mixed + other
                mixed = mixed + other
                fresh = mixed * 0.2 - learn_rate * grad.astype(F32)
                master[layer, part, :] = fresh
                copies[later, layer, part, :] = fresh.astype(BF16)

            @pl.when(layer > 0)
            def _():
                cast_one = copies[slot, layer, :width, :]
                for rows_ds in blocks:
                    d_normed = dot(d_pre[rows_ds, :], cast_one, 1, 1).astype(BF16).astype(F32)
                    inv = inv_rms[layer, rows_ds, :]
                    normed_f = hidden[layer, rows_ds, :].astype(F32) * inv
                    along = jnp.mean(d_normed * normed_f, axis=-1, keepdims=True)
                    d_in = inv * (d_normed - normed_f * along)
                    d_hid[rows_ds, :] = (d_hid[rows_ds, :].astype(F32) + d_in).astype(BF16)

            @pl.when(step + 1 < steps)
            def _():
                for copy in sends(later, layer):
                    copy.start()

            @pl.when(step + 1 == steps)
            def _():
                stage[layer] = master[layer, width:, :].T
                for copy in out_copies(layer):
                    copy.start()

            return inner

        lax.fori_loop(0, layers, backward_body, 0)
        return carry

    lax.fori_loop(0, steps, step_body, 0)

    def last_body(layer, carry):
        for copy in sends((steps - 1) % 2, layer):
            copy.wait_send()
        for copy in out_copies(layer):
            copy.wait()
        return carry

    lax.fori_loop(0, layers, last_body, 0)


def solution(mesh):
    grid_x = mesh.shape["tx"]

    def device_train(w_one, w_two, inputs, targets):
        layers, width, ffn = w_one.shape[2:]
        steps, rows = inputs.shape[2:4]
        block = min(256, rows)
        dims = (grid_x, steps, layers, rows, width, ffn, block)
        any_spec = pl.BlockSpec(memory_space=pl.ANY)
        out_one, out_two, losses = pl.pallas_call(
            functools.partial(train_kernel, dims),
            out_shape=(
                jax.ShapeDtypeStruct((layers, width, ffn), F32),
                jax.ShapeDtypeStruct((layers, ffn, width), F32),
                jax.ShapeDtypeStruct((steps,), F32),
            ),
            in_specs=[any_spec] * 4,
            out_specs=(any_spec, any_spec, pl.BlockSpec(memory_space=pltpu.SMEM)),
            scratch_shapes=[
                pltpu.VMEM((layers, 2 * width, ffn), F32),
                pltpu.VMEM((2, layers, 2 * width, ffn), BF16),
                pltpu.VMEM((3, 2, layers, 2 * width, ffn), BF16),
                pltpu.VMEM((layers + 1, rows, width), BF16),
                pltpu.VMEM((layers, rows, width), BF16),
                pltpu.VMEM((layers, rows, width), F32),
                pltpu.VMEM((layers, rows, ffn), BF16),
                pltpu.VMEM((layers, rows, ffn), F32),
                pltpu.VMEM((rows, width), BF16),
                pltpu.VMEM((rows, ffn), BF16),
                pltpu.VMEM((rows, width), BF16),
                pltpu.VMEM((layers, ffn, width), F32),
                pltpu.SemaphoreType.DMA((2, layers)),
                pltpu.SemaphoreType.DMA((2,)),
                pltpu.SemaphoreType.DMA((3, 2, layers)),
                pltpu.SemaphoreType.DMA((3, 2, layers)),
                pltpu.SemaphoreType.DMA((2, layers)),
            ],
            compiler_params=pltpu.CompilerParams(
                collective_id=0, has_side_effects=True, vmem_limit_bytes=62 * 1024 * 1024
            ),
            name="gossip_train",
        )(w_one[0, 0], w_two[0, 0], inputs[0, 0], targets[0, 0])
        return out_one[None, None], out_two[None, None], losses[None, None]

    grid_spec = P("tx", "ty")
    return jax.shard_map(
        device_train,
        mesh=mesh,
        in_specs=(grid_spec, grid_spec, grid_spec, grid_spec),
        out_specs=(grid_spec, grid_spec, grid_spec),
        check_vma=False,
    )
```

time: 849 us -> 289 us (0.34); the launches traced: 833 us -> 288 us
  matrix products: 510 us -> 0 us
  Pallas kernels: 0 us -> 283 us
  waiting for transfers between devices: 94.4 us -> 0 us
  other arithmetic: 90 us -> 0 us
  starting transfers between devices: 85.3 us -> 0 us
  local copies, waits for them, and re-layouts: 41.8 us -> 4.54 us
  between operations: 11.8 us -> 0.65 us
    dot_general x272 -> x0, matrix products: 510 us -> none  [the longest x40 106 us: local_grads(): jnp.einsum('bd,fd->bf', d_hidden, cast_two[layer_idx], preferred_element_...]
    pallas_call x0 -> x1, Pallas kernels: none -> 283 us  [device_train(): pl.pallas_call(functools.partial(train_kernel, dims), out_shape=(jax.Shap...]
    ppermute x48 -> x0, waiting for transfers between devices: 94.4 us -> none  [gossip(): lax.ppermute(cast_copy, axis_name, perm_pairs)]
    ppermute x48 -> x0, starting transfers between devices: 85.3 us -> none  [gossip(): lax.ppermute(cast_copy, axis_name, perm_pairs)]
    convert_element_type x48 -> x0, other arithmetic: 66.8 us -> none  [the longest x8 29.5 us: device_train(): cast_one = p_one.astype(jnp.bfloat16)]
    unnamed x728 -> x7, local copies, waits for them, and re-layouts: 38.6 us -> 4.54 us
    reduce_sum x16 -> x0, other arithmetic: 10.5 us -> none  [the longest x8 6.11 us: local_grads(): step_loss = jnp.mean(error_term * error_term)]
    broadcast_in_dim x2 -> x0, other arithmetic: 9.53 us -> none  [the longest x1 4.95 us: device_train(): p_one[None, None]]
  transfers between devices with their start and end apart: 48 -> 0, of which waited for: 8 -> 0; matrix products, arithmetic and copies ran while one was open for 74% -> 0% of each run, Pallas kernels for 0% -> 0%
where the time goes in v1:
time: 289 us; the launch traced here: 288 us
  Pallas kernels  283 us (98%)
  local copies, waits for them, and re-layouts  4.54 us (2%)
    pallas_call x1, Pallas kernels, device_train(): pl.pallas_call(functools.partial(train_kernel, dims), out_shape=(jax.Shap...  283 us

profile of v1, /device:TPU:1, one launch (start us, length us, event | category | flops | bytes accessed | tf_op | source)
XLA Modules:
  0.0 288.2 jit_solution(12584579687634077809)
XLA Ops:
  0.6 283.0 %gossip_train.1 = (f32[6,128,512]{2,1,0:T(8,128)}, f32[6,512,128]{2,1,0:T(8,128)}, f32[8]{0:T(128)}) custom-call(f32[6,128,512]{2,1,0:T(8,128)} %bitcast.9, f32[6,512,128]{2,1,0:T(8,128)} %bitcast.10, bf16[8,1024,128]{2,1,0:T(8,128)(2,1)} %bitcast.7, bf16[8,1024,128]{2,1,0:T(8,128)(2,1)} %bitcast.8), custom_call_target="tpu_custom_call" | custom-call | tf_op jit(solution)/shard_map/gossip_train/pallas_call | solution.py:215
  283.7 0.0 copy-start
  283.7 2.9 copy.10
  286.5 0.0 copy-done
  286.5 0.0 copy-start.1
  286.5 1.1 copy.11
  287.7 0.0 copy-done.1
  287.7 0.5 copy.12
Async XLA Ops:
  283.7 2.9 %copy-start = (f32[6,512,128]{2,1,0:T(8,128)S(1)}, f32[6,512,128]{2,1,0:T(8,128)}, u32[]{:S(2)}) copy-start(f32[6,512,128]{2,1,0:T(8,128)} %get-tuple-element.7) | copy-start | bytes 4718596
  286.5 1.1 copy-start.1

commit v2 on v1

--- a/solution.py
+++ b/solution.py
@@ -22,9 +22,9 @@
 def train_kernel(
     dims,
     w_one, w_two, inputs, targets,
-    out_one, out_two, losses,
-    master, copies, recv, hidden, normed, inv_rms, act, slope, d_hid, d_pre, goals, stage,
-    load_sem, data_sem, send_sem, recv_sem, out_sem,
+    master_one, stage, losses,
+    master_two, copies, recv, hidden, normed, inv_rms, act, slope, d_hid, d_pre, goals,
+    load_sem, data_sem, send_sem, recv_sem, entry_sem,
 ):
     grid_x, steps, layers, rows, width, ffn, block = dims
     learn_rate = width / (ffn * layers)
@@ -37,34 +37,42 @@
 
     def load_copies(layer):
         return (
-            pltpu.make_async_copy(w_one.at[layer], master.at[layer, pl.ds(0, width)], load_sem.at[0, layer]),
+            pltpu.make_async_copy(w_one.at[layer], master_one.at[layer], load_sem.at[0, layer]),
             pltpu.make_async_copy(w_two.at[layer], stage.at[layer], load_sem.at[1, layer]),
         )
 
-    def out_copies(layer):
-        return (
-            pltpu.make_async_copy(master.at[layer, pl.ds(0, width)], out_one.at[layer], out_sem.at[0, layer]),
-            pltpu.make_async_copy(stage.at[layer], out_two.at[layer], out_sem.at[1, layer]),
-        )
-
     def acts_copy(step):
         return pltpu.make_async_copy(inputs.at[step], hidden.at[0], data_sem.at[0])
 
     def goals_copy(step):
         return pltpu.make_async_copy(targets.at[step], goals, data_sem.at[1])
 
-    def sends(slot, layer):
+    def sends(slot, layer, peer_ids=(0, 1, 2)):
         return [
             pltpu.make_async_remote_copy(
                 src_ref=copies.at[slot, layer],
                 dst_ref=recv.at[peer_idx, slot, layer],
                 send_sem=send_sem.at[peer_idx, slot, layer],
                 recv_sem=recv_sem.at[peer_idx, slot, layer],
-                device_id=peer,
+                device_id=peers[peer_idx],
                 device_id_type=MESH,
             )
-            for peer_idx, peer in enumerate(peers)
+            for peer_idx in peer_ids
         ]
+
+    def start_sends(slot, layer, peer_ids=(0, 1, 2)):
+        for copy in sends(slot, layer, peer_ids):
+            copy.start()
+
+    is_first = me_x == 0
+    is_last = me_x == grid_x - 1
+    barrier = pltpu.get_barrier_semaphore()
+    pl.semaphore_signal(barrier, inc=1, device_id=peers[1], device_id_type=MESH)
+    pl.semaphore_signal(barrier, inc=1, device_id=peers[2], device_id_type=MESH)
+
+    @pl.when(jnp.logical_not(is_last))
+    def _():
+        pl.semaphore_signal(barrier, inc=1, device_id=peers[0], device_id_type=MESH)
 
     for layer in reversed(range(layers)):
         for copy in load_copies(layer):
@@ -72,24 +80,41 @@
     acts_copy(0).start()
     goals_copy(0).start()
 
-    barrier = pltpu.get_barrier_semaphore()
-    for peer in peers:
-        pl.semaphore_signal(barrier, inc=1, device_id=peer, device_id_type=MESH)
-    pl.semaphore_wait(barrier, 3)
+    pl.semaphore_wait(barrier, jnp.where(is_first, 2, 3))
+
+    @pl.when(is_last)
+    def _():
+        pl.semaphore_signal(entry_sem, inc=1, device_id=peers[0], device_id_type=MESH)
 
     def first_body(idx, carry):
         layer = layers - 1 - idx
         for copy in load_copies(layer):
             copy.wait()
-        copies[0, layer, :width, :] = master[layer, :width, :].astype(BF16)
+        copies[0, layer, :width, :] = master_one[layer].astype(BF16)
         turned = stage[layer].T
-        master[layer, width:, :] = turned
+        master_two[layer] = turned
         copies[0, layer, width:, :] = turned.astype(BF16)
-        for copy in sends(0, layer):
-            copy.start()
+        start_sends(0, layer, (0, 2))
+
+        @pl.when(jnp.logical_not(is_first))
+        def _():
+            start_sends(0, layer, (1,))
+
         return carry
 
     lax.fori_loop(0, layers, first_body, 0)
+
+    @pl.when(is_first)
+    def _():
+        pl.semaphore_wait(entry_sem, 1)
+
+        def late_body(idx, carry):
+            start_sends(0, layers - 1 - idx, (1,))
+            return carry
+
+        lax.fori_loop(0, layers, late_body, 0)
+
+    losses[...] = jnp.zeros(losses.shape, F32)
 
     def step_body(step, carry):
         slot = lax.rem(step, 2)
@@ -130,7 +155,9 @@
             error_term = hidden[layers, rows_ds, :].astype(F32) - goals[rows_ds, :].astype(F32)
             d_hid[rows_ds, :] = (error_term * (2.0 / (rows * width))).astype(BF16)
             total = total + jnp.sum((error_term * error_term).reshape(block // 8, 8, width), axis=0)
-        losses[step] = jnp.sum(total) / (rows * width)
+        step_loss = jnp.sum(total) / (rows * width)
+        lane = lax.broadcasted_iota(jnp.int32, losses.shape, 1)
+        losses[...] = jnp.where(lane == step, step_loss, losses[...])
 
         @pl.when(step + 1 < steps)
         def _():
@@ -153,15 +180,15 @@
                 for copy in sends(later, layer):
                     copy.wait_send()
 
-            for start, grad in ((0, grad_one), (width, grad_two)):
+            for start, grad, master in ((0, grad_one, master_one), (width, grad_two, master_two)):
                 part = pl.ds(start, width)
                 other = recv[2, slot, layer, part, :].astype(F32)
-                mixed = master[layer, part, :] + recv[0, slot, layer, part, :].astype(F32)
+                mixed = master[layer] + recv[0, slot, layer, part, :].astype(F32)
                 mixed = mixed + recv[1, slot, layer, part, :].astype(F32)
                 mixed = mixed + other
                 mixed = mixed + other
                 fresh = mixed * 0.2 - learn_rate * grad.astype(F32)
-                master[layer, part, :] = fresh
+                master[layer] = fresh
                 copies[later, layer, part, :] = fresh.astype(BF16)
 
             @pl.when(layer > 0)
@@ -177,14 +204,11 @@
 
             @pl.when(step + 1 < steps)
             def _():
-                for copy in sends(later, layer):
-                    copy.start()
+                start_sends(later, layer)
 
             @pl.when(step + 1 == steps)
             def _():
-                stage[layer] = master[layer, width:, :].T
-                for copy in out_copies(layer):
-                    copy.start()
+                stage[layer] = master_two[layer].T
 
             return inner
 
@@ -196,11 +220,20 @@
     def last_body(layer, carry):
         for copy in sends((steps - 1) % 2, layer):
             copy.wait_send()
-        for copy in out_copies(layer):
-            copy.wait()
         return carry
 
     lax.fori_loop(0, layers, last_body, 0)
+
+
+def write_kernel(one, two, losses, out_one, out_two, out_losses, sems):
+    copies = [
+        pltpu.make_async_copy(src, dst, sems.at[idx])
+        for idx, (src, dst) in enumerate(((one, out_one), (two, out_two), (losses, out_losses)))
+    ]
+    for copy in copies:
+        copy.start()
+    for copy in copies:
+        copy.wait()
 
 
 def solution(mesh):
@@ -212,17 +245,15 @@
         block = min(256, rows)
         dims = (grid_x, steps, layers, rows, width, ffn, block)
         any_spec = pl.BlockSpec(memory_space=pl.ANY)
-        out_one, out_two, losses = pl.pallas_call(
+        vmem_spec = pl.BlockSpec(memory_space=pltpu.VMEM)
+        shapes = ((layers, width, ffn), (layers, ffn, width), (1, steps))
+        one, two, losses = pl.pallas_call(
             functools.partial(train_kernel, dims),
-            out_shape=(
-                jax.ShapeDtypeStruct((layers, width, ffn), F32),
-                jax.ShapeDtypeStruct((layers, ffn, width), F32),
-                jax.ShapeDtypeStruct((steps,), F32),
-            ),
+            out_shape=tuple(pltpu.VMEM(shape, F32) for shape in shapes),
             in_specs=[any_spec] * 4,
-            out_specs=(any_spec, any_spec, pl.BlockSpec(memory_space=pltpu.SMEM)),
+            out_specs=(vmem_spec,) * 3,
             scratch_shapes=[
-                pltpu.VMEM((layers, 2 * width, ffn), F32),
+                pltpu.VMEM((layers, width, ffn), F32),
                 pltpu.VMEM((2, layers, 2 * width, ffn), BF16),
                 pltpu.VMEM((3, 2, layers, 2 * width, ffn), BF16),
                 pltpu.VMEM((layers + 1, rows, width), BF16),
@@ -233,19 +264,27 @@
                 pltpu.VMEM((rows, width), BF16),
                 pltpu.VMEM((rows, ffn), BF16),
                 pltpu.VMEM((rows, width), BF16),
-                pltpu.VMEM((layers, ffn, width), F32),
                 pltpu.SemaphoreType.DMA((2, layers)),
                 pltpu.SemaphoreType.DMA((2,)),
                 pltpu.SemaphoreType.DMA((3, 2, layers)),
                 pltpu.SemaphoreType.DMA((3, 2, layers)),
-                pltpu.SemaphoreType.DMA((2, layers)),
+                pltpu.SemaphoreType.REGULAR,
             ],
             compiler_params=pltpu.CompilerParams(
-                collective_id=0, has_side_effects=True, vmem_limit_bytes=62 * 1024 * 1024
+                collective_id=0, has_side_effects=True, vmem_limit_bytes=52 * 1024 * 1024
             ),
             name="gossip_train",
         )(w_one[0, 0], w_two[0, 0], inputs[0, 0], targets[0, 0])
-        return out_one[None, None], out_two[None, None], losses[None, None]
+        out_one, out_two, out_losses = pl.pallas_call(
+            write_kernel,
+            out_shape=tuple(jax.ShapeDtypeStruct(shape, F32) for shape in shapes),
+            in_specs=[vmem_spec] * 3,
+            out_specs=(any_spec,) * 3,
+            scratch_shapes=[pltpu.SemaphoreType.DMA((3,))],
+            compiler_params=pltpu.CompilerParams(vmem_limit_bytes=1024 * 1024),
+            name="write_out",
+        )(one, two, losses)
+        return out_one[None, None], out_two[None, None], out_losses[None]
 
     grid_spec = P("tx", "ty")
     return jax.shard_map(

time: 289 us -> 285 us (0.986)
  local copies, waits for them, and re-layouts: 4.54 us -> 0 us
    unnamed x7 -> x0, local copies, waits for them, and re-layouts: 4.54 us -> none
    pallas_call x1 -> x2, Pallas kernels: 283 us -> 283 us  [the longest x1 282 us: device_train(): pl.pallas_call(functools.partial(train_kernel, dims), out_shape=tuple((pl...]
where the time goes in v2:
time: 285 us; the launch traced here: 284 us
  Pallas kernels  283 us (99%)
    pallas_call x1, Pallas kernels, device_train(): pl.pallas_call(functools.partial(train_kernel, dims), out_shape=tuple((pl...  282 us

profile of v2, /device:TPU:1, one launch (start us, length us, event | category | flops | bytes accessed | tf_op | source)
XLA Modules:
  0.0 284.1 jit_solution(3184401825499485154)
XLA Ops:
  0.6 281.7 %gossip_train.1 = (f32[6,128,512]{2,1,0:T(8,128)S(1)}, f32[6,512,128]{2,1,0:T(8,128)S(1)}, f32[1,8]{1,0:T(1,128)S(1)}) custom-call(f32[6,128,512]{2,1,0:T(8,128)} %bitcast.9, f32[6,512,128]{2,1,0:T(8,128)} %bitcast.10, bf16[8,1024,128]{2,1,0:T(8,128)(2,1)} %bitcast.7, bf16[8,1024,128]{2,1,0:T(8,128)(2,1)} %bitcast.8), custom_call_target="tpu_custom_call" | custom-call | tf_op jit(solution)/shard_map/gossip_train/pallas_call | solution.py:250
  282.4 1.7 write_out.1

commit v3 on v2

--- a/solution.py
+++ b/solution.py
@@ -23,8 +23,8 @@
     dims,
     w_one, w_two, inputs, targets,
     master_one, stage, losses,
-    master_two, copies, recv, hidden, normed, inv_rms, act, slope, d_hid, d_pre, goals,
-    load_sem, data_sem, send_sem, recv_sem, entry_sem,
+    master_two, copies, recv, hidden, normed, inv_rms, act, slope, d_hid, d_pre, goals, relay,
+    load_sem, data_sem, send_sem, recv_sem, relay_sem, entry_sem,
 ):
     grid_x, steps, layers, rows, width, ffn, block = dims
     learn_rate = width / (ffn * layers)
@@ -64,55 +64,135 @@
         for copy in sends(slot, layer, peer_ids):
             copy.start()
 
-    is_first = me_x == 0
-    is_last = me_x == grid_x - 1
-    barrier = pltpu.get_barrier_semaphore()
-    pl.semaphore_signal(barrier, inc=1, device_id=peers[1], device_id_type=MESH)
-    pl.semaphore_signal(barrier, inc=1, device_id=peers[2], device_id_type=MESH)
-
-    @pl.when(jnp.logical_not(is_last))
-    def _():
-        pl.semaphore_signal(barrier, inc=1, device_id=peers[0], device_id_type=MESH)
-
-    for layer in reversed(range(layers)):
-        for copy in load_copies(layer):
-            copy.start()
-    acts_copy(0).start()
-    goals_copy(0).start()
-
-    pl.semaphore_wait(barrier, jnp.where(is_first, 2, 3))
-
-    @pl.when(is_last)
-    def _():
-        pl.semaphore_signal(entry_sem, inc=1, device_id=peers[0], device_id_type=MESH)
-
-    def first_body(idx, carry):
-        layer = layers - 1 - idx
+    near, far = (4, 8) if grid_x >= 32 else (2, 3)
+    offset = jnp.where(me_y == 0, near, far)
+    first, last = 0, grid_x - 1
+    low_relay, high_relay = first + offset, last - offset
+    is_first, is_last = me_x == first, me_x == last
+    is_low, is_high = me_x == low_relay, me_x == high_relay
+    up_rows, down_rows = 3 * width // 2, width
+
+    def at_x(index):
+        return {"tx": index}
+
+    def direct_part(peer_idx, start):
+        part = pl.ds(start, 2 * width - start)
+        return pltpu.make_async_remote_copy(
+            src_ref=copies.at[0, 0, part],
+            dst_ref=recv.at[peer_idx, 0, 0, part],
+            send_sem=send_sem.at[peer_idx, 0, 0],
+            recv_sem=recv_sem.at[peer_idx, 0, 0],
+            device_id=peers[peer_idx],
+            device_id_type=MESH,
+        )
+
+    def to_relay(peer_idx, size, index):
+        return pltpu.make_async_remote_copy(
+            src_ref=copies.at[0, 0, pl.ds(0, size)],
+            dst_ref=relay.at[pl.ds(0, size)],
+            send_sem=send_sem.at[peer_idx, 0, 0],
+            recv_sem=relay_sem.at[0],
+            device_id=at_x(index),
+            device_id_type=MESH,
+        )
+
+    def from_relay(peer_idx, size, index):
+        return pltpu.make_async_remote_copy(
+            src_ref=relay.at[pl.ds(0, size)],
+            dst_ref=recv.at[peer_idx, 0, 0, pl.ds(0, size)],
+            send_sem=relay_sem.at[1],
+            recv_sem=recv_sem.at[peer_idx, 0, 0],
+            device_id=at_x(index),
+            device_id_type=MESH,
+        )
+
+    def cast_layer(layer):
         for copy in load_copies(layer):
             copy.wait()
         copies[0, layer, :width, :] = master_one[layer].astype(BF16)
         turned = stage[layer].T
         master_two[layer] = turned
         copies[0, layer, width:, :] = turned.astype(BF16)
-        start_sends(0, layer, (0, 2))
+
+    def first_sends(layer):
+        start_sends(0, layer, (2,))
+        by_relay = jnp.logical_and(is_last, layer == 0)
+
+        @pl.when(jnp.logical_not(by_relay))
+        def _():
+            start_sends(0, layer, (0,))
+
+        @pl.when(by_relay)
+        def _():
+            to_relay(0, up_rows, high_relay).start()
+            direct_part(0, up_rows).start()
 
         @pl.when(jnp.logical_not(is_first))
         def _():
             start_sends(0, layer, (1,))
 
+    for copy in load_copies(layers - 1):
+        copy.start()
+
+    barrier = pltpu.get_barrier_semaphore()
+
+    def announce(peer):
+        pl.semaphore_signal(barrier, inc=1, device_id=peer, device_id_type=MESH)
+
+    announce(peers[1])
+    announce(peers[2])
+
+    @pl.when(jnp.logical_not(is_last))
+    def _():
+        announce(peers[0])
+
+    @pl.when(is_first)
+    def _():
+        announce(at_x(high_relay))
+
+    @pl.when(is_low)
+    def _():
+        announce(at_x(first))
+        announce(at_x(last))
+
+    @pl.when(is_high)
+    def _():
+        announce(at_x(last))
+
+    cast_layer(layers - 1)
+    pl.semaphore_wait(barrier, 3 + 2 * is_last.astype(jnp.int32) + is_high.astype(jnp.int32))
+    first_sends(layers - 1)
+
+    for layer in reversed(range(layers - 1)):
+        for copy in load_copies(layer):
+            copy.start()
+    acts_copy(0).start()
+    goals_copy(0).start()
+
+    @pl.when(is_last)
+    def _():
+        for index in (first, low_relay):
+            pl.semaphore_signal(entry_sem, inc=1, device_id=at_x(index), device_id_type=MESH)
+
+    def first_body(idx, carry):
+        layer = layers - 1 - idx
+        cast_layer(layer)
+        first_sends(layer)
         return carry
 
-    lax.fori_loop(0, layers, first_body, 0)
+    lax.fori_loop(1, layers, first_body, 0)
 
     @pl.when(is_first)
     def _():
+        to_relay(1, down_rows, low_relay).start()
         pl.semaphore_wait(entry_sem, 1)
 
         def late_body(idx, carry):
             start_sends(0, layers - 1 - idx, (1,))
             return carry
 
-        lax.fori_loop(0, layers, late_body, 0)
+        lax.fori_loop(0, layers - 1, late_body, 0)
+        direct_part(1, down_rows).start()
 
     losses[...] = jnp.zeros(losses.shape, F32)
 
@@ -149,6 +229,17 @@
         def _():
             acts_copy(step + 1).start()
 
+        @pl.when(jnp.logical_and(step == 0, is_high))
+        def _():
+            to_relay(0, up_rows, high_relay).wait_recv()
+            from_relay(0, up_rows, first).start()
+
+        @pl.when(jnp.logical_and(step == 0, is_low))
+        def _():
+            to_relay(1, down_rows, low_relay).wait_recv()
+            pl.semaphore_wait(entry_sem, 1)
+            from_relay(1, down_rows, last).start()
+
         goals_copy(step).wait()
         total = jnp.zeros((8, width), F32)
         for rows_ds in blocks:
@@ -223,6 +314,14 @@
         return carry
 
     lax.fori_loop(0, layers, last_body, 0)
+
+    @pl.when(is_high)
+    def _():
+        from_relay(0, up_rows, first).wait_send()
+
+    @pl.when(is_low)
+    def _():
+        from_relay(1, down_rows, last).wait_send()
 
 
 def write_kernel(one, two, losses, out_one, out_two, out_losses, sems):
@@ -264,10 +363,12 @@
                 pltpu.VMEM((rows, width), BF16),
                 pltpu.VMEM((rows, ffn), BF16),
                 pltpu.VMEM((rows, width), BF16),
+                pltpu.VMEM((2 * width, ffn), BF16),
                 pltpu.SemaphoreType.DMA((2, layers)),
                 pltpu.SemaphoreType.DMA((2,)),
                 pltpu.SemaphoreType.DMA((3, 2, layers)),
                 pltpu.SemaphoreType.DMA((3, 2, layers)),
+                pltpu.SemaphoreType.DMA((2,)),
                 pltpu.SemaphoreType.REGULAR,
             ],
             compiler_params=pltpu.CompilerParams(

time: 285 us -> 327 us (1.15); the launches traced: 284 us -> 322 us
  Pallas kernels: 283 us -> 322 us
    pallas_call x1, Pallas kernels: 282 us -> 320 us  [device_train(): pl.pallas_call(functools.partial(train_kernel, dims), out_shape=tuple((pl...]
where the time goes in v3:
time: 327 us; the launch traced here: 322 us
  Pallas kernels  322 us (98%)
    pallas_call x1, Pallas kernels, device_train(): pl.pallas_call(functools.partial(train_kernel, dims), out_shape=tuple((pl...  320 us

profile of v3, /device:TPU:1, one launch (start us, length us, event | category | flops | bytes accessed | tf_op | source)
XLA Modules:
  0.0 322.4 jit_solution(15437081938000050417)
XLA Ops:
  0.6 320.0 %gossip_train.1 = (f32[6,128,512]{2,1,0:T(8,128)S(1)}, f32[6,512,128]{2,1,0:T(8,128)S(1)}, f32[1,8]{1,0:T(1,128)S(1)}) custom-call(f32[6,128,512]{2,1,0:T(8,128)} %bitcast.9, f32[6,512,128]{2,1,0:T(8,128)} %bitcast.10, bf16[8,1024,128]{2,1,0:T(8,128)(2,1)} %bitcast.7, bf16[8,1024,128]{2,1,0:T(8,128)(2,1)} %bitcast.8), custom_call_target="tpu_custom_call" | custom-call | tf_op jit(solution)/shard_map/gossip_train/pallas_call | solution.py:349
  320.7 1.7 write_out.1

commit v4 on v3

--- a/solution.py
+++ b/solution.py
@@ -71,6 +71,7 @@
     is_first, is_last = me_x == first, me_x == last
     is_low, is_high = me_x == low_relay, me_x == high_relay
     up_rows, down_rows = 3 * width // 2, width
+    top = layers - 1
 
     def at_x(index):
         return {"tx": index}
@@ -78,19 +79,19 @@
     def direct_part(peer_idx, start):
         part = pl.ds(start, 2 * width - start)
         return pltpu.make_async_remote_copy(
-            src_ref=copies.at[0, 0, part],
-            dst_ref=recv.at[peer_idx, 0, 0, part],
-            send_sem=send_sem.at[peer_idx, 0, 0],
-            recv_sem=recv_sem.at[peer_idx, 0, 0],
+            src_ref=copies.at[0, top, part],
+            dst_ref=recv.at[peer_idx, 0, top, part],
+            send_sem=send_sem.at[peer_idx, 0, top],
+            recv_sem=recv_sem.at[peer_idx, 0, top],
             device_id=peers[peer_idx],
             device_id_type=MESH,
         )
 
     def to_relay(peer_idx, size, index):
         return pltpu.make_async_remote_copy(
-            src_ref=copies.at[0, 0, pl.ds(0, size)],
+            src_ref=copies.at[0, top, pl.ds(0, size)],
             dst_ref=relay.at[pl.ds(0, size)],
-            send_sem=send_sem.at[peer_idx, 0, 0],
+            send_sem=send_sem.at[peer_idx, 0, top],
             recv_sem=relay_sem.at[0],
             device_id=at_x(index),
             device_id_type=MESH,
@@ -99,9 +100,9 @@
     def from_relay(peer_idx, size, index):
         return pltpu.make_async_remote_copy(
             src_ref=relay.at[pl.ds(0, size)],
-            dst_ref=recv.at[peer_idx, 0, 0, pl.ds(0, size)],
+            dst_ref=recv.at[peer_idx, 0, top, pl.ds(0, size)],
             send_sem=relay_sem.at[1],
-            recv_sem=recv_sem.at[peer_idx, 0, 0],
+            recv_sem=recv_sem.at[peer_idx, 0, top],
             device_id=at_x(index),
             device_id_type=MESH,
         )
@@ -115,23 +116,13 @@
         copies[0, layer, width:, :] = turned.astype(BF16)
 
     def first_sends(layer):
-        start_sends(0, layer, (2,))
-        by_relay = jnp.logical_and(is_last, layer == 0)
-
-        @pl.when(jnp.logical_not(by_relay))
-        def _():
-            start_sends(0, layer, (0,))
-
-        @pl.when(by_relay)
-        def _():
-            to_relay(0, up_rows, high_relay).start()
-            direct_part(0, up_rows).start()
+        start_sends(0, layer, (0, 2))
 
         @pl.when(jnp.logical_not(is_first))
         def _():
             start_sends(0, layer, (1,))
 
-    for copy in load_copies(layers - 1):
+    for copy in load_copies(top):
         copy.start()
 
     barrier = pltpu.get_barrier_semaphore()
@@ -159,11 +150,24 @@
     def _():
         announce(at_x(last))
 
-    cast_layer(layers - 1)
+    cast_layer(top)
     pl.semaphore_wait(barrier, 3 + 2 * is_last.astype(jnp.int32) + is_high.astype(jnp.int32))
-    first_sends(layers - 1)
-
-    for layer in reversed(range(layers - 1)):
+
+    @pl.when(is_last)
+    def _():
+        to_relay(0, up_rows, high_relay).start()
+        direct_part(0, up_rows).start()
+        start_sends(0, top, (1, 2))
+
+    @pl.when(is_first)
+    def _():
+        to_relay(1, down_rows, low_relay).start()
+
+    @pl.when(jnp.logical_not(is_last))
+    def _():
+        first_sends(top)
+
+    for layer in reversed(range(top)):
         for copy in load_copies(layer):
             copy.start()
     acts_copy(0).start()
@@ -175,8 +179,20 @@
             pl.semaphore_signal(entry_sem, inc=1, device_id=at_x(index), device_id_type=MESH)
 
     def first_body(idx, carry):
-        layer = layers - 1 - idx
+        layer = top - idx
         cast_layer(layer)
+
+        @pl.when(jnp.logical_and(idx == layers // 2, is_high))
+        def _():
+            to_relay(0, up_rows, high_relay).wait_recv()
+            from_relay(0, up_rows, first).start()
+
+        @pl.when(jnp.logical_and(idx == layers // 2, is_low))
+        def _():
+            to_relay(1, down_rows, low_relay).wait_recv()
+            pl.semaphore_wait(entry_sem, 1)
+            from_relay(1, down_rows, last).start()
+
         first_sends(layer)
         return carry
 
@@ -184,15 +200,14 @@
 
     @pl.when(is_first)
     def _():
-        to_relay(1, down_rows, low_relay).start()
         pl.semaphore_wait(entry_sem, 1)
+        direct_part(1, down_rows).start()
 
         def late_body(idx, carry):
-            start_sends(0, layers - 1 - idx, (1,))
+            start_sends(0, top - idx, (1,))
             return carry
 
-        lax.fori_loop(0, layers - 1, late_body, 0)
-        direct_part(1, down_rows).start()
+        lax.fori_loop(1, layers, late_body, 0)
 
     losses[...] = jnp.zeros(losses.shape, F32)
 
@@ -228,17 +243,6 @@
         @pl.when(step + 1 < steps)
         def _():
             acts_copy(step + 1).start()
-
-        @pl.when(jnp.logical_and(step == 0, is_high))
-        def _():
-            to_relay(0, up_rows, high_relay).wait_recv()
-            from_relay(0, up_rows, first).start()
-
-        @pl.when(jnp.logical_and(step == 0, is_low))
-        def _():
-            to_relay(1, down_rows, low_relay).wait_recv()
-            pl.semaphore_wait(entry_sem, 1)
-            from_relay(1, down_rows, last).start()
 
         goals_copy(step).wait()
         total = jnp.zeros((8, width), F32)

time: 327 us -> 329 us (level); the launches traced: 322 us -> 329 us
  Pallas kernels: 322 us -> 328 us
    pallas_call x1, Pallas kernels: 320 us -> 326 us  [device_train(): pl.pallas_call(functools.partial(train_kernel, dims), out_shape=tuple((pl...]
where the time goes in v4:
time: 329 us
  Pallas kernels  328 us (100%)
    pallas_call x1, Pallas kernels, device_train(): pl.pallas_call(functools.partial(train_kernel, dims), out_shape=tuple((pl...  326 us

profile of v4, /device:TPU:1, one launch (start us, length us, event | category | flops | bytes accessed | tf_op | source)
XLA Modules:
  0.0 328.7 jit_solution(8508121600328168278)
XLA Ops:
  0.6 326.4 %gossip_train.1 = (f32[6,128,512]{2,1,0:T(8,128)S(1)}, f32[6,512,128]{2,1,0:T(8,128)S(1)}, f32[1,8]{1,0:T(1,128)S(1)}) custom-call(f32[6,128,512]{2,1,0:T(8,128)} %bitcast.9, f32[6,512,128]{2,1,0:T(8,128)} %bitcast.10, bf16[8,1024,128]{2,1,0:T(8,128)(2,1)} %bitcast.7, bf16[8,1024,128]{2,1,0:T(8,128)(2,1)} %bitcast.8), custom_call_target="tpu_custom_call" | custom-call | tf_op jit(solution)/shard_map/gossip_train/pallas_call | solution.py:353
  327.0 1.7 write_out.1

commit v5 on v4

--- a/solution.py
+++ b/solution.py
@@ -64,13 +64,11 @@
         for copy in sends(slot, layer, peer_ids):
             copy.start()
 
-    near, far = (4, 8) if grid_x >= 32 else (2, 3)
-    offset = jnp.where(me_y == 0, near, far)
     first, last = 0, grid_x - 1
-    low_relay, high_relay = first + offset, last - offset
+    up_relay, down_relay = first + 3, last - 3
     is_first, is_last = me_x == first, me_x == last
-    is_low, is_high = me_x == low_relay, me_x == high_relay
-    up_rows, down_rows = 3 * width // 2, width
+    is_up, is_down = me_x == up_relay, me_x == down_relay
+    up_rows, down_rows = 9 * width // 8, 5 * width // 8
     top = layers - 1
 
     def at_x(index):
@@ -139,29 +137,21 @@
 
     @pl.when(is_first)
     def _():
-        announce(at_x(high_relay))
-
-    @pl.when(is_low)
-    def _():
-        announce(at_x(first))
+        announce(at_x(up_relay))
+
+    @pl.when(jnp.logical_or(is_up, is_down))
+    def _():
         announce(at_x(last))
 
-    @pl.when(is_high)
-    def _():
-        announce(at_x(last))
-
     cast_layer(top)
-    pl.semaphore_wait(barrier, 3 + 2 * is_last.astype(jnp.int32) + is_high.astype(jnp.int32))
+    extra = 2 * is_last.astype(jnp.int32) + is_up.astype(jnp.int32) - is_first.astype(jnp.int32)
+    pl.semaphore_wait(barrier, 3 + extra)
 
     @pl.when(is_last)
     def _():
-        to_relay(0, up_rows, high_relay).start()
+        to_relay(0, up_rows, up_relay).start()
         direct_part(0, up_rows).start()
         start_sends(0, top, (1, 2))
-
-    @pl.when(is_first)
-    def _():
-        to_relay(1, down_rows, low_relay).start()
 
     @pl.when(jnp.logical_not(is_last))
     def _():
@@ -175,22 +165,20 @@
 
     @pl.when(is_last)
     def _():
-        for index in (first, low_relay):
-            pl.semaphore_signal(entry_sem, inc=1, device_id=at_x(index), device_id_type=MESH)
+        pl.semaphore_signal(entry_sem, inc=1, device_id=peers[0], device_id_type=MESH)
 
     def first_body(idx, carry):
         layer = top - idx
         cast_layer(layer)
 
-        @pl.when(jnp.logical_and(idx == layers // 2, is_high))
-        def _():
-            to_relay(0, up_rows, high_relay).wait_recv()
+        @pl.when(jnp.logical_and(idx == layers // 2, is_up))
+        def _():
+            to_relay(0, up_rows, up_relay).wait_recv()
             from_relay(0, up_rows, first).start()
 
-        @pl.when(jnp.logical_and(idx == layers // 2, is_low))
-        def _():
-            to_relay(1, down_rows, low_relay).wait_recv()
-            pl.semaphore_wait(entry_sem, 1)
+        @pl.when(jnp.logical_and(idx == layers // 2, is_down))
+        def _():
+            to_relay(1, down_rows, down_relay).wait_recv()
             from_relay(1, down_rows, last).start()
 
         first_sends(layer)
@@ -201,6 +189,7 @@
     @pl.when(is_first)
     def _():
         pl.semaphore_wait(entry_sem, 1)
+        to_relay(1, down_rows, down_relay).start()
         direct_part(1, down_rows).start()
 
         def late_body(idx, carry):
@@ -319,11 +308,11 @@
 
     lax.fori_loop(0, layers, last_body, 0)
 
-    @pl.when(is_high)
+    @pl.when(is_up)
     def _():
         from_relay(0, up_rows, first).wait_send()
 
-    @pl.when(is_low)
+    @pl.when(is_down)
     def _():
         from_relay(1, down_rows, last).wait_send()
 

time: 329 us -> 282 us (0.86)
  Pallas kernels: 328 us -> 280 us
    pallas_call x1, Pallas kernels: 326 us -> 279 us  [device_train(): pl.pallas_call(functools.partial(train_kernel, dims), out_shape=tuple((pl...]
where the time goes in v5:
time: 282 us; the launch traced here: 281 us
  Pallas kernels  280 us (99%)
    pallas_call x1, Pallas kernels, device_train(): pl.pallas_call(functools.partial(train_kernel, dims), out_shape=tuple((pl...  279 us

profile of v5, /device:TPU:1, one launch (start us, length us, event | category | flops | bytes accessed | tf_op | source)
XLA Modules:
  0.0 281.0 jit_solution(8826542253965695734)
XLA Ops:
  0.6 278.6 %gossip_train.1 = (f32[6,128,512]{2,1,0:T(8,128)S(1)}, f32[6,512,128]{2,1,0:T(8,128)S(1)}, f32[1,8]{1,0:T(1,128)S(1)}) custom-call(f32[6,128,512]{2,1,0:T(8,128)} %bitcast.9, f32[6,512,128]{2,1,0:T(8,128)} %bitcast.10, bf16[8,1024,128]{2,1,0:T(8,128)(2,1)} %bitcast.7, bf16[8,1024,128]{2,1,0:T(8,128)(2,1)} %bitcast.8), custom_call_target="tpu_custom_call" | custom-call | tf_op jit(solution)/shard_map/gossip_train/pallas_call | solution.py:342
  279.3 1.7 write_out.1

commit v6 on v5

--- a/solution.py
+++ b/solution.py
@@ -64,15 +64,24 @@
         for copy in sends(slot, layer, peer_ids):
             copy.start()
 
-    first, last = 0, grid_x - 1
-    up_relay, down_relay = first + 3, last - 3
-    is_first, is_last = me_x == first, me_x == last
-    is_up, is_down = me_x == up_relay, me_x == down_relay
-    up_rows, down_rows = 9 * width // 8, 5 * width // 8
+    plane, near, far = (16, 3, 7) if grid_x >= 32 else (8, 2, 3)
+    place = lax.rem(me_x, plane)
+    ring_first, ring_last = me_x == 0, me_x == grid_x - 1
+    is_first, is_last = place == 0, place == plane - 1
+    is_up, is_down = place == near, place == plane - 1 - near
+    low_end, high_end = me_x < plane, me_x >= grid_x - plane
+    is_up_far, is_down_far = me_x == far, me_x == grid_x - 1 - far
+    turn_rows, up_rows, down_rows = 3 * width // 8, 3 * width // 4, width // 2
     top = layers - 1
 
-    def at_x(index):
-        return {"tx": index}
+    def both(one, two):
+        return jnp.logical_and(one, two)
+
+    def no(flag):
+        return jnp.logical_not(flag)
+
+    def shifted(offset):
+        return {"tx": lax.rem(me_x + offset + grid_x, grid_x)}
 
     def direct_part(peer_idx, start):
         part = pl.ds(start, 2 * width - start)
@@ -85,25 +94,84 @@
             device_id_type=MESH,
         )
 
-    def to_relay(peer_idx, size, index):
+    def to_relay(peer_idx, size):
         return pltpu.make_async_remote_copy(
             src_ref=copies.at[0, top, pl.ds(0, size)],
             dst_ref=relay.at[pl.ds(0, size)],
             send_sem=send_sem.at[peer_idx, 0, top],
             recv_sem=relay_sem.at[0],
-            device_id=at_x(index),
+            device_id=shifted((1 + near, -1 - near)[peer_idx]),
             device_id_type=MESH,
         )
 
-    def from_relay(peer_idx, size, index):
+    def pass_on(peer_idx, size):
+        part = pl.ds(size, size)
         return pltpu.make_async_remote_copy(
-            src_ref=relay.at[pl.ds(0, size)],
-            dst_ref=recv.at[peer_idx, 0, top, pl.ds(0, size)],
+            src_ref=relay.at[part],
+            dst_ref=relay.at[part],
+            send_sem=relay_sem.at[2],
+            recv_sem=relay_sem.at[0],
+            device_id=shifted((far - near, near - far)[peer_idx]),
+            device_id_type=MESH,
+        )
+
+    def from_relay(peer_idx, start, size, distance):
+        part = pl.ds(start, size)
+        return pltpu.make_async_remote_copy(
+            src_ref=relay.at[part],
+            dst_ref=recv.at[peer_idx, 0, top, part],
             send_sem=relay_sem.at[1],
             recv_sem=recv_sem.at[peer_idx, 0, top],
-            device_id=at_x(index),
+            device_id=shifted((-distance, distance)[peer_idx]),
             device_id_type=MESH,
         )
+
+    relays = (
+        (0, is_up, low_end, is_up_far, up_rows),
+        (1, is_down, high_end, is_down_far, down_rows),
+    )
+
+    def relay_near():
+        for peer_idx, is_near, is_end, _, size in relays:
+
+            @pl.when(both(is_near, is_end))
+            def _():
+                to_relay(peer_idx, 2 * size).wait_recv()
+                pass_on(peer_idx, size).start()
+                from_relay(peer_idx, 0, size, near).start()
+
+            @pl.when(both(is_near, no(is_end)))
+            def _():
+                to_relay(peer_idx, turn_rows).wait_recv()
+                from_relay(peer_idx, 0, turn_rows, near).start()
+
+    def relay_far():
+        for peer_idx, _, _, is_far, size in relays:
+
+            @pl.when(is_far)
+            def _():
+                pass_on(peer_idx, size).wait_recv()
+                from_relay(peer_idx, size, size, far).start()
+
+    def relay_end():
+        for peer_idx, is_near, is_end, is_far, size in relays:
+
+            @pl.when(both(is_near, is_end))
+            def _():
+                pass_on(peer_idx, size).wait_send()
+                from_relay(peer_idx, 0, size, near).wait_send()
+
+            @pl.when(both(is_near, no(is_end)))
+            def _():
+                from_relay(peer_idx, 0, turn_rows, near).wait_send()
+
+            @pl.when(is_far)
+            def _():
+                from_relay(peer_idx, size, size, far).wait_send()
+
+    def turn_sends(peer_idx, size):
+        to_relay(peer_idx, size).start()
+        direct_part(peer_idx, size).start()
 
     def cast_layer(layer):
         for copy in load_copies(layer):
@@ -116,7 +184,7 @@
     def first_sends(layer):
         start_sends(0, layer, (0, 2))
 
-        @pl.when(jnp.logical_not(is_first))
+        @pl.when(no(ring_first))
         def _():
             start_sends(0, layer, (1,))
 
@@ -131,31 +199,61 @@
     announce(peers[1])
     announce(peers[2])
 
-    @pl.when(jnp.logical_not(is_last))
+    @pl.when(no(ring_last))
     def _():
         announce(peers[0])
 
     @pl.when(is_first)
     def _():
-        announce(at_x(up_relay))
-
-    @pl.when(jnp.logical_or(is_up, is_down))
-    def _():
-        announce(at_x(last))
+        announce(shifted(near))
+
+    @pl.when(is_up)
+    def _():
+        announce(shifted(-1 - near))
+
+    @pl.when(both(is_down, high_end))
+    def _():
+        announce(shifted(near))
+
+    @pl.when(both(is_down, no(high_end)))
+    def _():
+        announce(shifted(1 + near))
+
+    @pl.when(is_up_far)
+    def _():
+        announce(shifted(near - far))
+
+    @pl.when(is_down_far)
+    def _():
+        announce(shifted(far - near))
 
     cast_layer(top)
-    extra = 2 * is_last.astype(jnp.int32) + is_up.astype(jnp.int32) - is_first.astype(jnp.int32)
-    pl.semaphore_wait(barrier, 3 + extra)
-
-    @pl.when(is_last)
-    def _():
-        to_relay(0, up_rows, up_relay).start()
-        direct_part(0, up_rows).start()
-        start_sends(0, top, (1, 2))
-
-    @pl.when(jnp.logical_not(is_last))
-    def _():
-        first_sends(top)
+    expected = 3
+    for flag in (is_first, is_last, ring_last, is_up, both(is_up, low_end), both(is_down, high_end)):
+        expected = expected + flag.astype(jnp.int32)
+    pl.semaphore_wait(barrier, expected - 2 * ring_first.astype(jnp.int32))
+
+    start_sends(0, top, (2,))
+
+    @pl.when(ring_last)
+    def _():
+        turn_sends(0, 2 * up_rows)
+
+    @pl.when(both(is_last, no(ring_last)))
+    def _():
+        turn_sends(0, turn_rows)
+
+    @pl.when(no(is_last))
+    def _():
+        start_sends(0, top, (0,))
+
+    @pl.when(both(is_first, no(ring_first)))
+    def _():
+        turn_sends(1, turn_rows)
+
+    @pl.when(no(is_first))
+    def _():
+        start_sends(0, top, (1,))
 
     for layer in reversed(range(top)):
         for copy in load_copies(layer):
@@ -163,7 +261,7 @@
     acts_copy(0).start()
     goals_copy(0).start()
 
-    @pl.when(is_last)
+    @pl.when(ring_last)
     def _():
         pl.semaphore_signal(entry_sem, inc=1, device_id=peers[0], device_id_type=MESH)
 
@@ -171,26 +269,23 @@
         layer = top - idx
         cast_layer(layer)
 
-        @pl.when(jnp.logical_and(idx == layers // 2, is_up))
+        @pl.when(idx == layers // 2)
         def _():
-            to_relay(0, up_rows, up_relay).wait_recv()
-            from_relay(0, up_rows, first).start()
-
-        @pl.when(jnp.logical_and(idx == layers // 2, is_down))
+            relay_near()
+
+        @pl.when(idx == (layers + 2) // 2)
         def _():
-            to_relay(1, down_rows, down_relay).wait_recv()
-            from_relay(1, down_rows, last).start()
+            relay_far()
 
         first_sends(layer)
         return carry
 
     lax.fori_loop(1, layers, first_body, 0)
 
-    @pl.when(is_first)
+    @pl.when(ring_first)
     def _():
         pl.semaphore_wait(entry_sem, 1)
-        to_relay(1, down_rows, down_relay).start()
-        direct_part(1, down_rows).start()
+        turn_sends(1, 2 * down_rows)
 
         def late_body(idx, carry):
             start_sends(0, top - idx, (1,))
@@ -308,13 +403,7 @@
 
     lax.fori_loop(0, layers, last_body, 0)
 
-    @pl.when(is_up)
-    def _():
-        from_relay(0, up_rows, first).wait_send()
-
-    @pl.when(is_down)
-    def _():
-        from_relay(1, down_rows, last).wait_send()
+    relay_end()
 
 
 def write_kernel(one, two, losses, out_one, out_two, out_losses, sems):
@@ -361,7 +450,7 @@
                 pltpu.SemaphoreType.DMA((2,)),
                 pltpu.SemaphoreType.DMA((3, 2, layers)),
                 pltpu.SemaphoreType.DMA((3, 2, layers)),
-                pltpu.SemaphoreType.DMA((2,)),
+                pltpu.SemaphoreType.DMA((3,)),
                 pltpu.SemaphoreType.REGULAR,
             ],
             compiler_params=pltpu.CompilerParams(

time: 282 us -> 281 us (level)
  no operation moved by 1% of the time
where the time goes in v6:
time: 281 us
  Pallas kernels  280 us (100%)
    pallas_call x1, Pallas kernels, device_train(): pl.pallas_call(functools.partial(train_kernel, dims), out_shape=tuple((pl...  279 us

profile of v6, /device:TPU:1, one launch (start us, length us, event | category | flops | bytes accessed | tf_op | source)
XLA Modules:
  0.0 280.9 jit_solution(10307441727284142027)
XLA Ops:
  0.6 278.6 %gossip_train.1 = (f32[6,128,512]{2,1,0:T(8,128)S(1)}, f32[6,512,128]{2,1,0:T(8,128)S(1)}, f32[1,8]{1,0:T(1,128)S(1)}) custom-call(f32[6,128,512]{2,1,0:T(8,128)} %bitcast.9, f32[6,512,128]{2,1,0:T(8,128)} %bitcast.10, bf16[8,1024,128]{2,1,0:T(8,128)(2,1)} %bitcast.7, bf16[8,1024,128]{2,1,0:T(8,128)(2,1)} %bitcast.8), custom_call_target="tpu_custom_call" | custom-call | tf_op jit(solution)/shard_map/gossip_train/pallas_call | solution.py:431
  279.2 1.7 write_out.1

commit v7 on v6

--- a/solution.py
+++ b/solution.py
@@ -24,7 +24,7 @@
     w_one, w_two, inputs, targets,
     master_one, stage, losses,
     master_two, copies, recv, hidden, normed, inv_rms, act, slope, d_hid, d_pre, goals, relay,
-    load_sem, data_sem, send_sem, recv_sem, relay_sem, entry_sem,
+    load_sem, data_sem, send_sem, recv_sem, relay_sem, tail_sem, entry_sem,
 ):
     grid_x, steps, layers, rows, width, ffn, block = dims
     learn_rate = width / (ffn * layers)
@@ -58,6 +58,21 @@
                 device_id_type=MESH,
             )
             for peer_idx in peer_ids
+        ]
+
+    def tail_half(part):
+        slot = (steps - 1) % 2
+        half = pl.ds(part * width, width)
+        return [
+            pltpu.make_async_remote_copy(
+                src_ref=copies.at[slot, 0, half],
+                dst_ref=recv.at[peer_idx, slot, 0, half],
+                send_sem=tail_sem.at[0, peer_idx, part],
+                recv_sem=tail_sem.at[1, peer_idx, part],
+                device_id=peer,
+                device_id_type=MESH,
+            )
+            for peer_idx, peer in enumerate(peers)
         ]
 
     def start_sends(slot, layer, peer_ids=(0, 1, 2)):
@@ -351,15 +366,24 @@
             grad_two = dot(d_hid[...], act[layer], 0, 0).astype(BF16)
             grad_one = dot(normed[layer], d_pre[...], 0, 0).astype(BF16)
 
-            for copy in sends(slot, layer):
-                copy.wait_recv()
+            is_tail = both(step + 1 == steps, layer == 0)
+
+            @pl.when(no(is_tail))
+            def _():
+                for copy in sends(slot, layer):
+                    copy.wait_recv()
+
+            @pl.when(is_tail)
+            def _():
+                for copy in tail_half(1):
+                    copy.wait_recv()
 
             @pl.when(step > 0)
             def _():
                 for copy in sends(later, layer):
                     copy.wait_send()
 
-            for start, grad, master in ((0, grad_one, master_one), (width, grad_two, master_two)):
+            def update(start, grad, master):
                 part = pl.ds(start, width)
                 other = recv[2, slot, layer, part, :].astype(F32)
                 mixed = master[layer] + recv[0, slot, layer, part, :].astype(F32)
@@ -370,6 +394,19 @@
                 master[layer] = fresh
                 copies[later, layer, part, :] = fresh.astype(BF16)
 
+            update(width, grad_two, master_two)
+
+            @pl.when(step + 1 == steps)
+            def _():
+                stage[layer] = master_two[layer].T
+
+            @pl.when(is_tail)
+            def _():
+                for copy in tail_half(0):
+                    copy.wait_recv()
+
+            update(0, grad_one, master_one)
+
             @pl.when(layer > 0)
             def _():
                 cast_one = copies[slot, layer, :width, :]
@@ -381,13 +418,16 @@
                     d_in = inv * (d_normed - normed_f * along)
                     d_hid[rows_ds, :] = (d_hid[rows_ds, :].astype(F32) + d_in).astype(BF16)
 
-            @pl.when(step + 1 < steps)
+            to_tail = both(step + 2 == steps, layer == 0)
+
+            @pl.when(both(step + 1 < steps, no(to_tail)))
             def _():
                 start_sends(later, layer)
 
-            @pl.when(step + 1 == steps)
-            def _():
-                stage[layer] = master_two[layer].T
+            @pl.when(to_tail)
+            def _():
+                for copy in tail_half(1) + tail_half(0):
+                    copy.start()
 
             return inner
 
@@ -401,16 +441,18 @@
             copy.wait_send()
         return carry
 
-    lax.fori_loop(0, layers, last_body, 0)
+    lax.fori_loop(1, layers, last_body, 0)
+    for copy in tail_half(1) + tail_half(0):
+        copy.wait_send()
 
     relay_end()
 
 
 def write_kernel(one, two, losses, out_one, out_two, out_losses, sems):
-    copies = [
-        pltpu.make_async_copy(src, dst, sems.at[idx])
-        for idx, (src, dst) in enumerate(((one, out_one), (two, out_two), (losses, out_losses)))
-    ]
+    pairs = [(losses, out_losses)]
+    for layer in range(one.shape[0]):
+        pairs += [(one.at[layer], out_one.at[layer]), (two.at[layer], out_two.at[layer])]
+    copies = [pltpu.make_async_copy(src, dst, sems.at[idx]) for idx, (src, dst) in enumerate(pairs)]
     for copy in copies:
         copy.start()
     for copy in copies:
@@ -451,6 +493,7 @@
                 pltpu.SemaphoreType.DMA((3, 2, layers)),
                 pltpu.SemaphoreType.DMA((3, 2, layers)),
                 pltpu.SemaphoreType.DMA((3,)),
+                pltpu.SemaphoreType.DMA((2, 3, 2)),
                 pltpu.SemaphoreType.REGULAR,
             ],
             compiler_params=pltpu.CompilerParams(
@@ -463,7 +506,7 @@
             out_shape=tuple(jax.ShapeDtypeStruct(shape, F32) for shape in shapes),
             in_specs=[vmem_spec] * 3,
             out_specs=(any_spec,) * 3,
-            scratch_shapes=[pltpu.SemaphoreType.DMA((3,))],
+            scratch_shapes=[pltpu.SemaphoreType.DMA((2 * layers + 1,))],
             compiler_params=pltpu.CompilerParams(vmem_limit_bytes=1024 * 1024),
             name="write_out",
         )(one, two, losses)

time: 281 us -> 281 us (level)
  no operation moved by 1% of the time
where the time goes in v7:
time: 281 us
  Pallas kernels  280 us (100%)
    pallas_call x1, Pallas kernels, device_train(): pl.pallas_call(functools.partial(train_kernel, dims), out_shape=tuple((pl...  279 us

profile of v7, /device:TPU:1, one launch (start us, length us, event | category | flops | bytes accessed | tf_op | source)
XLA Modules:
  0.0 280.9 jit_solution(5566152179403735562)
XLA Ops:
  0.6 278.5 %gossip_train.1 = (f32[6,128,512]{2,1,0:T(8,128)S(1)}, f32[6,512,128]{2,1,0:T(8,128)S(1)}, f32[1,8]{1,0:T(1,128)S(1)}) custom-call(f32[6,128,512]{2,1,0:T(8,128)} %bitcast.9, f32[6,512,128]{2,1,0:T(8,128)} %bitcast.10, bf16[8,1024,128]{2,1,0:T(8,128)(2,1)} %bitcast.7, bf16[8,1024,128]{2,1,0:T(8,128)(2,1)} %bitcast.8), custom_call_target="tpu_custom_call" | custom-call | tf_op jit(solution)/shard_map/gossip_train/pallas_call | solution.py:473
  279.2 1.8 write_out.1

commit v8 on v7

--- a/solution.py
+++ b/solution.py
@@ -449,10 +449,10 @@
 
 
 def write_kernel(one, two, losses, out_one, out_two, out_losses, sems):
-    pairs = [(losses, out_losses)]
-    for layer in range(one.shape[0]):
-        pairs += [(one.at[layer], out_one.at[layer]), (two.at[layer], out_two.at[layer])]
-    copies = [pltpu.make_async_copy(src, dst, sems.at[idx]) for idx, (src, dst) in enumerate(pairs)]
+    copies = [
+        pltpu.make_async_copy(src, dst, sems.at[idx])
+        for idx, (src, dst) in enumerate(((one, out_one), (two, out_two), (losses, out_losses)))
+    ]
     for copy in copies:
         copy.start()
     for copy in copies:
@@ -506,7 +506,7 @@
             out_shape=tuple(jax.ShapeDtypeStruct(shape, F32) for shape in shapes),
             in_specs=[vmem_spec] * 3,
             out_specs=(any_spec,) * 3,
-            scratch_shapes=[pltpu.SemaphoreType.DMA((2 * layers + 1,))],
+            scratch_shapes=[pltpu.SemaphoreType.DMA((3,))],
             compiler_params=pltpu.CompilerParams(vmem_limit_bytes=1024 * 1024),
             name="write_out",
         )(one, two, losses)

time: 281 us -> 281 us (level)
  no operation moved by 1% of the time
where the time goes in v8:
time: 281 us
  Pallas kernels  280 us (100%)
    pallas_call x1, Pallas kernels, device_train(): pl.pallas_call(functools.partial(train_kernel, dims), out_shape=tuple((pl...  279 us

profile of v8, /device:TPU:1, one launch (start us, length us, event | category | flops | bytes accessed | tf_op | source)
XLA Modules:
  0.0 280.9 jit_solution(11486247102295338280)
XLA Ops:
  0.6 278.5 %gossip_train.1 = (f32[6,128,512]{2,1,0:T(8,128)S(1)}, f32[6,512,128]{2,1,0:T(8,128)S(1)}, f32[1,8]{1,0:T(1,128)S(1)}) custom-call(f32[6,128,512]{2,1,0:T(8,128)} %bitcast.9, f32[6,512,128]{2,1,0:T(8,128)} %bitcast.10, bf16[8,1024,128]{2,1,0:T(8,128)(2,1)} %bitcast.7, bf16[8,1024,128]{2,1,0:T(8,128)(2,1)} %bitcast.8), custom_call_target="tpu_custom_call" | custom-call | tf_op jit(solution)/shard_map/gossip_train/pallas_call | solution.py:473
  279.2 1.7 write_out.1
